TPU v7x, 256 devices: a whole 4x4x8 slice. The times are simulated.
256 devices in a mesh: dom: 256 (over y, x, z, core).
Axes of the slice: x: 4, y: 4, z: 8, core: 2. Of those that a mesh axis runs over, the one named last changes fastest.
Arguments:
- displacement: float32 [8, 3, 524288], P(None, None, 'dom'), may hold values from -1.5 to 1.5
- adjoint_disp: float32 [8, 3, 524288], P(None, None, 'dom'), may hold values from -1.5 to 1.5
- pressure: float32 [8, 524288], P(None, 'dom'), may hold values from -3 to 3
- adjoint_pressure: float32 [8, 524288], P(None, 'dom'), may hold values from -3 to 3
- youngs: float32 [524288], P('dom'), may hold values from 0.5 to 2
- permeability: float32 [524288], P('dom'), may hold values from 0.3 to 3
- stiffness: float32 [24, 24], replicated
- send_nodes: int32 [8, 32768], P(None, 'dom'), may hold values from 0 to 2047
- send_cells: int32 [8, 32768], P(None, 'dom'), may hold values from 0 to 2047
- elem_nodes: int32 [8, 524288], P(None, 'dom'), may hold values from 0 to 3071, as said below
- inner_faces: int32 [2, 1572864], P(None, 'dom'), may hold values from 0 to 2047
- cross_faces: int32 [2, 262144], P(None, 'dom'), may hold values from 0 to 2047, as said below
Outputs:
- grad_log_youngs: float32 [524288], P('dom')
- grad_log_perm: float32 [524288], P('dom')
Inputs may be any that keep to these rules, and one draw needn't show every extreme that they name: `send_cells`: entries refer to the partition's own cells; block j of partition c is read by partition c - o_j. `elem_nodes`: The first 1536 elements of each partition name only its own nodes; corner 0 of each of the last 512 is a ghost node. `cross_faces`: row 0 is an own cell; row 1 is j * 128 + g with d + o_j always on the axis. `inner_faces`: both rows name cells of the same partition.
All inputs are finite; a program needn't handle non-finite values.
Results may differ from a plain program's by a relative error of at most 0.0003.
Values sent between devices are 32-bit elements; how exact they have to be, the bound alone decides.
No kernel may reach another device: no remote copies, remote signals or barrier semaphores. Data moves between devices by JAX's collectives and lax.ppermute only.
A program may use at most 192 MiB of HBM per device.

v0:
```python
import jax
import jax.numpy as jnp
from jax import lax
from jax.experimental import pallas as pl
from jax.experimental.pallas import tpu as pltpu
from jax.sharding import PartitionSpec as P


OFFSETS = (1, -1, 2, -2, 4, -4, 8, -8)
SLOTS = 8
STEPS = 8
EL = 2048
EB = 512
OWN = EL - EB
FI = 6144
FX = 1024
LANES = 128
OWN_CHUNKS = EL // LANES
NODE_ROWS = 6 * STEPS
FACE_ROW = NODE_ROWS + 24
FACE_K = FACE_ROW + 16 * (FX // LANES)
FACE_ID = FACE_K + 8
ROWS = FACE_ID + 8
VMEM = pltpu.CompilerParams(vmem_limit_bytes=48 * 2**20)


def lane_take(table, lo):
    return jnp.take_along_axis(table, lo, axis=1, mode="promise_in_bounds")


def split_index(row):
    wide = jnp.broadcast_to(row, (8, LANES))
    return wide & (LANES - 1), wide >> 7


def select_rows(tables, lo, hi, chunks):
    picked = [lane_take(table(0), lo) for table in tables]
    for chunk in range(1, chunks):
        here = hi == chunk
        picked = [jnp.where(here, lane_take(table(chunk), lo), old) for table, old in zip(tables, picked)]
    return picked


def select_scalar(blocks, lo, hi):
    sub = lax.broadcasted_iota(jnp.int32, (8, LANES), 0)
    total = None
    for number, block in enumerate(blocks):
        part = jnp.where(hi == sub + 8 * number, lane_take(block, lo), 0.0)
        total = part if total is None else total + part
    return jnp.sum(total, axis=0, keepdims=True)


def cell_tables(p_ref, q_ref):
    return [
        lambda h: p_ref[:, h * LANES : (h + 1) * LANES],
        lambda h: q_ref[:, h * LANES : (h + 1) * LANES],
    ]


def node_tables(d_ref, a_ref):
    def table(ref, comp):
        return lambda h: ref[comp, :, h * LANES : (h + 1) * LANES]

    return [table(d_ref, comp) for comp in range(3)] + [table(a_ref, comp) for comp in range(3)]


def face_terms(pa, qa, ka, pb, qb, kb):
    product = jnp.sum((pa - pb) * (qa - qb), axis=0, keepdims=True)
    total = ka + kb
    common = 2.0 * ka * kb * product / (total * total)
    return common * kb, common * ka


def scatter(index, term):
    length = index.shape[1]
    lo = index & (LANES - 1)
    hi = index >> 7
    hot = jnp.where(lax.broadcasted_iota(jnp.int32, (LANES, length), 0) == lo, 1.0, 0.0).astype(jnp.bfloat16)
    top = term.astype(jnp.bfloat16).astype(jnp.float32)
    rows = lax.broadcasted_iota(jnp.int32, (16, length), 0) == hi
    left = jnp.concatenate([jnp.where(rows, top, 0.0), jnp.where(rows, term - top, 0.0)], axis=0)
    out = lax.dot_general(
        left.astype(jnp.bfloat16), hot, (((1,), (1,)), ((), ())), preferred_element_type=jnp.float32
    )
    return out[:16] + out[16:]


def halves(value):
    top = value.astype(jnp.bfloat16)
    return top, (value - top.astype(jnp.float32)).astype(jnp.bfloat16)


def spread_stiffness(k_ref):
    pick = (
        lax.broadcasted_iota(jnp.int32, (192, 24), 0) // 8 == lax.broadcasted_iota(jnp.int32, (192, 24), 1)
    ).astype(jnp.float32).astype(jnp.bfloat16)
    same = (lax.broadcasted_iota(jnp.int32, (192, 192), 0) & 7) == (
        lax.broadcasted_iota(jnp.int32, (192, 192), 1) & 7
    )
    out = []
    for half in halves(k_ref[...]):
        tall = jnp.dot(pick, half, preferred_element_type=jnp.float32).astype(jnp.bfloat16)
        full = lax.dot_general(tall, pick, (((1,), (1,)), ((), ())), preferred_element_type=jnp.float32)
        out.append(jnp.where(same, full, 0.0).astype(jnp.bfloat16))
    return out


def strain_of(k_ref, f_ref, a_ref):
    top, low = spread_stiffness(k_ref)
    f_top, f_low = halves(f_ref[...])
    weighted = jnp.dot(top, f_top, preferred_element_type=jnp.float32)
    weighted += jnp.dot(low, f_top, preferred_element_type=jnp.float32)
    weighted += jnp.dot(top, f_low, preferred_element_type=jnp.float32)
    return jnp.sum(a_ref[...] * weighted, axis=0, keepdims=True)


def fill_table(raw_ref, tab_ref, chunks, read):
    for chunk in range(chunks):
        for number in range(6):
            line = 48 * chunk + 8 * number
            raw_ref[line : line + 8, :] = read(number, chunk)
    top, low = halves(raw_ref[...])
    tab_ref[:, :LANES] = top
    tab_ref[:, LANES:] = low


def lookup(tab_ref, rows, first, last, olds=(None, None)):
    sub = lax.broadcasted_iota(jnp.int32, (LANES, LANES), 0)
    hot = jnp.concatenate(
        [jnp.where(sub == (row & (LANES - 1)), 1.0, 0.0).astype(jnp.bfloat16) for row in rows], axis=1
    )
    found = jnp.dot(tab_ref[...], jnp.concatenate([hot, hot], axis=0), preferred_element_type=jnp.float32)
    results = []
    for place, (row, old) in enumerate(zip(rows, olds)):
        hi = jnp.broadcast_to(row >> 7, (8, LANES))
        got = [None] * 6 if old is None else old
        for chunk in range(first, last):
            base = 48 * (chunk - first)
            new = [found[base + 8 * r : base + 8 * r + 8, place * LANES : (place + 1) * LANES] for r in range(6)]
            here = hi == chunk
            got = [fresh if kept is None else jnp.where(here, fresh, kept) for fresh, kept in zip(new, got)]
        results.append(got)
    return results


def lines(corner):
    return [(8 * comp + corner) * 8 for comp in range(3)]


def put(f_ref, a_ref, corner, cols, got):
    for comp, line in enumerate(lines(corner)):
        f_ref[line : line + 8, cols] = got[comp]
        a_ref[line : line + 8, cols] = got[3 + comp]


def own_corners(tab_ref, nodes, elem, pairs, lone, f_ref, a_ref, cols):
    for pair in pairs:
        for corner, got in zip(pair, lookup(tab_ref, [elem[n : n + 1] for n in pair], 0, OWN_CHUNKS)):
            put(f_ref, a_ref, corner, cols, got)
    for corner in lone:
        lo, hi = split_index(elem[corner : corner + 1])
        put(f_ref, a_ref, corner, cols, select_rows(nodes, lo, hi, OWN_CHUNKS))


def ghost_corners(tab_ref, elem, first, last, old_f, old_a, f_ref, a_ref, cols, fresh):
    for pair in range(4):
        corners = (2 * pair, 2 * pair + 1)
        olds = [
            None
            if corner == 0 and fresh
            else [ref[line : line + 8, cols] for ref in (old_f, old_a) for line in lines(corner)]
            for corner in corners
        ]
        for corner, got in zip(corners, lookup(tab_ref, [elem[n : n + 1] for n in corners], first, last, olds)):
            put(f_ref, a_ref, corner, cols, got)


SOURCES = 12


def pack_kernel(*refs):
    sources, outs, raw_s, sem = refs[:SOURCES], refs[SOURCES:-2], refs[-2], refs[-1]
    far_ref, near_refs, cells_ref, faces_ref = outs[0], outs[1 : NEAR + 1], outs[NEAR + 1], outs[NEAR + 2]
    tab_ref, local = outs[NEAR + 3], outs[NEAR + 4 :]
    copies = [pltpu.make_async_copy(far, near, sem.at[n]) for n, (far, near) in enumerate(zip(sources, local))]
    for copy in copies:
        copy.start()
    for copy in copies[:8]:
        copy.wait()
    p_ref, q_ref, k_ref, cf_ref, sc_ref, sn_ref, d_ref, a_ref = local[:8]
    nodes = node_tables(d_ref, a_ref)
    cells = cell_tables(p_ref, q_ref)
    perm = [k_ref[0:8, :], k_ref[8:16, :]]
    for m in range(FX // LANES):
        cols = slice(m * LANES, (m + 1) * LANES)
        lo, hi = split_index(cf_ref[0:1, cols])
        pa, qa = select_rows(cells, lo, hi, OWN_CHUNKS)
        ka = select_scalar(perm, lo, hi)
        slot = cf_ref[1:2, cols].astype(jnp.float32)
        for ref, base in [(one, FACE_ROW) for one in near_refs] + [(faces_ref, 0), (far_ref, FAR_FACES)]:
            ref[base + 16 * m : base + 16 * m + 8, :] = pa
            ref[base + 16 * m + 8 : base + 16 * m + 16, :] = qa
            ref[base + 128 + m : base + 129 + m, :] = ka
            ref[base + 136 + m : base + 137 + m, :] = slot
    fill_table(raw_s, tab_ref, OWN_CHUNKS, lambda number, chunk: nodes[number](chunk))
    for j in range(SLOTS):
        out, start = (near_refs[ORDER.index(j)], 0) if j < NEAR else (far_ref, BLOCK * (j - NEAR))
        if j % 2 == 0:
            both = lookup(tab_ref, [sn_ref[n : n + 1, :] for n in (j, j + 1)], 0, OWN_CHUNKS)
        for number, value in enumerate(both[j % 2]):
            out[start + 8 * number : start + 8 * number + 8, :] = value
        lo, hi = split_index(sc_ref[j : j + 1, :])
        pb, qb = select_rows(cells, lo, hi, OWN_CHUNKS)
        kb = jnp.broadcast_to(select_scalar(perm, lo, hi), (8, LANES))
        for ref, base in ((out, start + NODE_ROWS), (cells_ref, 24 * j)):
            ref[base : base + 8, :] = pb
            ref[base + 8 : base + 16, :] = qb
            ref[base + 16 : base + 24, :] = kb
    for copy in copies[8:]:
        copy.wait()


FACE_BLOCK = 6
EARLY = FI // FACE_BLOCK
ORDER = (2, 4, 0, 1, 5, 3)
NEAR = len(ORDER)
BLOCK = NODE_ROWS + 24
FAR_FACES = 2 * BLOCK
FAR_ROWS = FAR_FACES + 144


def inner_kernel(tab_ref, p_ref, q_ref, k_ref, y_ref, s_ref, en_ref, if_ref, gy_ref, gp_ref, f_s, a_s, t_s):
    cells = cell_tables(p_ref, q_ref)
    perm = [k_ref[0:8, :], k_ref[8:16, :]]
    width = FACE_BLOCK * LANES
    t_s[:, :width] = jnp.zeros((2, width), jnp.float32)

    def add(step, total):
        cols = pl.ds(pl.multiple_of(step * width, width), width)
        for side in range(2):
            total = total + scatter(if_ref[side : side + 1, cols], t_s[side : side + 1, cols])
        return total

    def block(step, total):
        total = add(jnp.maximum(step - 1, 0), total)
        cols = pl.ds(pl.multiple_of(step * LANES, LANES), LANES)
        elem = en_ref[:, cols]
        own_corners(tab_ref, None, elem, ((0, 1), (2, 3), (4, 5), (6, 7)), (), f_s, a_s, cols)
        for face in range(FACE_BLOCK):
            offset = pl.multiple_of(step * width + face * LANES, LANES)
            ends = []
            for side in range(2):
                lo, hi = split_index(if_ref[side : side + 1, pl.ds(offset, LANES)])
                ends += select_rows(cells, lo, hi, OWN_CHUNKS) + [select_scalar(perm, lo, hi)]
            term_a, term_b = face_terms(*ends)
            t_s[0:1, pl.ds(offset, LANES)] = term_a
            t_s[1:2, pl.ds(offset, LANES)] = term_b
        return total

    steps = FI // width
    total = lax.fori_loop(0, steps, block, jnp.zeros((16, LANES), jnp.float32))
    gp_ref[...] = add(steps - 1, total)
    gy_ref[...] = -y_ref[:, :EARLY] * strain_of(s_ref, f_s, a_s)


def edge_kernel(tab_ref, d_ref, a_ref, y_ref, s_ref, en_ref, gyi_ref, gy_ref, fo_ref, ao_ref, f_s, a_s):
    nodes = node_tables(d_ref, a_ref)

    def block(step, _):
        start = pl.multiple_of(step * LANES, LANES)
        cols = pl.ds(start, LANES)
        elem = en_ref[:, pl.ds(pl.multiple_of(EARLY + start, LANES), LANES)]
        own_corners(tab_ref, nodes, elem, ((0, 1), (2, 3), (4, 5)), (6, 7), f_s, a_s, cols)
        elem = en_ref[:, pl.ds(pl.multiple_of(OWN + start, LANES), LANES)]
        own_corners(tab_ref, nodes, elem, ((1, 2), (3, 4)), (5, 6, 7), fo_ref, ao_ref, cols)
        return 0

    lax.fori_loop(0, EB // LANES, block, 0)
    gy_ref[:, :EARLY] = gyi_ref[...]
    gy_ref[:, EARLY:] = -y_ref[:, EARLY:OWN] * strain_of(s_ref, f_s, a_s)


def incoming(got, cells_ref, sc_ref, slots, i_s, t_s, start):
    for number, j in enumerate(slots):
        mine = j ^ 1
        pt = cells_ref[24 * mine : 24 * mine + 8, :]
        qt = cells_ref[24 * mine + 8 : 24 * mine + 16, :]
        kt = cells_ref[24 * mine + 16 : 24 * mine + 24, :]
        place = jnp.broadcast_to(sc_ref[mine : mine + 1, :], (8, LANES))
        for m in range(FX // LANES):
            base = start + number * FX + m * LANES
            cols = slice(base, base + LANES)
            lo, hi = split_index(got[j][FACE_ID + m : FACE_ID + m + 1, :].astype(jnp.int32))
            pa = got[j][FACE_ROW + 16 * m : FACE_ROW + 16 * m + 8, :]
            qa = got[j][FACE_ROW + 16 * m + 8 : FACE_ROW + 16 * m + 16, :]
            ka = got[j][FACE_K + m : FACE_K + m + 1, :]
            kb = lane_take(kt, lo)[0:1]
            term = face_terms(pa, qa, ka, lane_take(pt, lo), lane_take(qt, lo), kb)[1]
            i_s[0:1, cols] = lane_take(place, lo)[0:1]
            t_s[0:1, cols] = jnp.where(hi[0:1] == mine, term, 0.0)


def add_terms(i_s, t_s, count, total):
    def add(step, total):
        cols = pl.ds(pl.multiple_of(step * 1024, 1024), 1024)
        return total + scatter(i_s[0:1, cols], t_s[0:1, cols])

    return lax.fori_loop(0, count, add, total)


def near_kernel(*refs):
    near, (fo_ref, ao_ref, cells_ref, sc_ref, en_ref, gpi_ref) = refs[:NEAR], refs[NEAR : NEAR + 6]
    f_ref, a_ref, gp_ref, i_s, t_s, raw_s, tab_s = refs[NEAR + 6 :]
    got = [near[ORDER.index(j)] for j in range(NEAR)]
    fill_table(raw_s, tab_s, NEAR, lambda number, chunk: got[chunk][8 * number : 8 * number + 8, :])
    for step in range(EB // LANES):
        elem = en_ref[:, OWN + step * LANES : OWN + (step + 1) * LANES]
        cols = slice(step * LANES, (step + 1) * LANES)
        ghost_corners(tab_s, elem, OWN_CHUNKS, OWN_CHUNKS + NEAR, fo_ref, ao_ref, f_ref, a_ref, cols, True)
    incoming(got, cells_ref, sc_ref, range(NEAR), i_s, t_s, 0)
    gp_ref[...] = add_terms(i_s, t_s, NEAR, gpi_ref[...])


def tail_kernel(*refs):
    near, (swapped, relayed) = refs[:NEAR], refs[NEAR : NEAR + 2]
    (fo_ref, ao_ref, cells_ref, faces_ref, y_ref, s_ref, sc_ref, en_ref, cf_ref, gyi_ref, gpi_ref) = refs[NEAR + 2 : NEAR + 13]
    gy_ref, gp_ref, f_s, a_s, i_s, t_s, raw_s, tab_s, up_s, down_s = refs[NEAR + 13 :]
    got = [near[ORDER.index(j)] for j in range(NEAR)] + [up_s, down_s]
    low = jnp.broadcast_to((lax.axis_index("dom") & 8) == 0, (8, LANES))
    for ref, start, direct, other in ((up_s, 0, swapped, relayed), (down_s, BLOCK, relayed, swapped)):
        for to, source, length in ((0, start, BLOCK), (BLOCK, FAR_FACES, 144)):
            for row in range(0, length, 8):
                ref[to + row : to + row + 8, :] = jnp.where(
                    low, direct[source + row : source + row + 8, :], other[source + row : source + row + 8, :]
                )
    fill_table(raw_s, tab_s, 2, lambda number, chunk: got[NEAR + chunk][8 * number : 8 * number + 8, :])
    for step in range(EB // LANES):
        elem = en_ref[:, OWN + step * LANES : OWN + (step + 1) * LANES]
        cols = slice(step * LANES, (step + 1) * LANES)
        ghost_corners(
            tab_s, elem, OWN_CHUNKS + NEAR, OWN_CHUNKS + SLOTS, fo_ref, ao_ref, f_s, a_s, cols, False
        )

    ghosts = [
        lambda h: got[h][NODE_ROWS : NODE_ROWS + 8, :],
        lambda h: got[h][NODE_ROWS + 8 : NODE_ROWS + 16, :],
    ]
    ghost_perm = jnp.concatenate([got[j][NODE_ROWS + 16 : NODE_ROWS + 17, :] for j in range(SLOTS)], axis=0)
    for m in range(FX // LANES):
        cols = slice(m * LANES, (m + 1) * LANES)
        lo, hi = split_index(cf_ref[1:2, cols])
        pb, qb = select_rows(ghosts, lo, hi, SLOTS)
        kb = select_scalar([ghost_perm], lo, hi)
        pa = faces_ref[16 * m : 16 * m + 8, :]
        qa = faces_ref[16 * m + 8 : 16 * m + 16, :]
        ka = faces_ref[128 + m : 129 + m, :]
        i_s[0:1, cols] = cf_ref[0:1, cols]
        t_s[0:1, cols] = face_terms(pa, qa, ka, pb, qb, kb)[0]
    incoming(got, cells_ref, sc_ref, (6, 7), i_s, t_s, FX)
    gp_ref[...] = add_terms(i_s, t_s, 3, gpi_ref[...])
    gy_ref[:, :OWN] = gyi_ref[...]
    gy_ref[:, OWN:] = -y_ref[:, OWN:] * strain_of(s_ref, f_s, a_s)


def shape(*dims):
    return jax.ShapeDtypeStruct(dims, jnp.float32)


def on_device(
    displacement,
    adjoint_disp,
    pressure,
    adjoint_pressure,
    youngs,
    permeability,
    stiffness,
    send_nodes,
    send_cells,
    elem_nodes,
    inner_faces,
    cross_faces,
):
    forward = displacement.transpose(1, 0, 2)
    adjoint = adjoint_disp.transpose(1, 0, 2)
    perm = permeability.reshape(OWN_CHUNKS, LANES)
    young = youngs.reshape(1, EL)
    sources = (
        pressure,
        adjoint_pressure,
        perm,
        cross_faces,
        send_cells,
        send_nodes,
        forward,
        adjoint,
        elem_nodes,
        inner_faces,
        young,
        stiffness,
    )
    packed = pl.pallas_call(
        pack_kernel,
        out_shape=[shape(FAR_ROWS, LANES)]
        + [shape(ROWS, LANES)] * NEAR
        + [shape(24 * SLOTS, LANES), shape(144, LANES)]
        + [jax.ShapeDtypeStruct((48 * OWN_CHUNKS, 2 * LANES), jnp.bfloat16)]
        + [jax.ShapeDtypeStruct(one.shape, one.dtype) for one in sources],
        in_specs=[pl.BlockSpec(memory_space=pltpu.HBM)] * SOURCES,
        scratch_shapes=[pltpu.VMEM((48 * OWN_CHUNKS, LANES), jnp.float32), pltpu.SemaphoreType.DMA((SOURCES,))],
        compiler_params=VMEM,
        name="pack",
    )(*(pltpu.with_memory_space_constraint(one, pltpu.HBM) for one in sources))
    cells, faces, table = packed[NEAR + 1 : NEAR + 4]
    (
        pressure,
        adjoint_pressure,
        perm,
        cross_faces,
        send_cells,
        _,
        forward,
        adjoint,
        elem_nodes,
        inner_faces,
        young,
        stiffness,
    ) = packed[NEAR + 4 :]
    count = lax.axis_size("dom")
    swapped = lax.ppermute(packed[0], "dom", [(source, source ^ 8) for source in range(count)])
    near = []
    for number, j in enumerate(ORDER):
        pairs = [(source, (source - OFFSETS[j]) % count) for source in range(count)]
        near.append(lax.ppermute(packed[number + 1], "dom", pairs))
    inner_young, inner_perm = pl.pallas_call(
        inner_kernel,
        out_shape=[shape(1, EARLY), shape(OWN_CHUNKS, LANES)],
        scratch_shapes=[
            pltpu.VMEM((192, EARLY), jnp.float32),
            pltpu.VMEM((192, EARLY), jnp.float32),
            pltpu.VMEM((2, FI), jnp.float32),
        ],
        compiler_params=VMEM,
        cost_estimate=pl.CostEstimate(flops=4 * 10**9, bytes_accessed=10**7, transcendentals=0),
        name="inner",
    )(table, pressure, adjoint_pressure, perm, young, stiffness, elem_nodes, inner_faces)
    swapped, inner_young, inner_perm, table = lax.optimization_barrier((swapped, inner_young, inner_perm, table))
    relayed = lax.ppermute(
        swapped, "dom", [(source, (source - 16 if source & 8 else source + 16) % count) for source in range(count)]
    )
    own_young, edge_forward, edge_adjoint = pl.pallas_call(
        edge_kernel,
        out_shape=[shape(1, OWN), shape(192, EB), shape(192, EB)],
        scratch_shapes=[pltpu.VMEM((192, EB), jnp.float32), pltpu.VMEM((192, EB), jnp.float32)],
        compiler_params=VMEM,
        cost_estimate=pl.CostEstimate(flops=2 * 10**9, bytes_accessed=10**7, transcendentals=0),
        name="edge",
    )(table, forward, adjoint, young, stiffness, elem_nodes, inner_young)
    edge_forward, edge_adjoint, near_perm = pl.pallas_call(
        near_kernel,
        out_shape=[shape(192, EB), shape(192, EB), shape(OWN_CHUNKS, LANES)],
        scratch_shapes=[
            pltpu.VMEM((1, NEAR * FX), jnp.int32),
            pltpu.VMEM((1, NEAR * FX), jnp.float32),
            pltpu.VMEM((48 * NEAR, LANES), jnp.float32),
            pltpu.VMEM((48 * NEAR, 2 * LANES), jnp.bfloat16),
        ],
        compiler_params=VMEM,
        name="near",
    )(*near, edge_forward, edge_adjoint, cells, send_cells, elem_nodes, inner_perm)
    grad_young, grad_perm = pl.pallas_call(
        tail_kernel,
        out_shape=[shape(1, EL), shape(OWN_CHUNKS, LANES)],
        scratch_shapes=[
            pltpu.VMEM((192, EB), jnp.float32),
            pltpu.VMEM((192, EB), jnp.float32),
            pltpu.VMEM((1, 3 * FX), jnp.int32),
            pltpu.VMEM((1, 3 * FX), jnp.float32),
            pltpu.VMEM((96, LANES), jnp.float32),
            pltpu.VMEM((96, 2 * LANES), jnp.bfloat16),
            pltpu.VMEM((ROWS, LANES), jnp.float32),
            pltpu.VMEM((ROWS, LANES), jnp.float32),
        ],
        compiler_params=VMEM,
        name="tail",
    )(
        *near,
        swapped,
        relayed,
        edge_forward,
        edge_adjoint,
        cells,
        faces,
        young,
        stiffness,
        send_cells,
        elem_nodes,
        cross_faces,
        own_young,
        near_perm,
    )
    return (grad_young.reshape(EL), grad_perm.reshape(EL))


def solution(mesh):
    in_specs = (
        P(None, None, "dom"),
        P(None, None, "dom"),
        P(None, "dom"),
        P(None, "dom"),
        P("dom"),
        P("dom"),
        P(),
        P(None, "dom"),
        P(None, "dom"),
        P(None, "dom"),
        P(None, "dom"),
        P(None, "dom"),
    )
    out_specs = (P("dom"), P("dom"))
    return jax.shard_map(
        on_device, mesh=mesh, in_specs=in_specs, out_specs=out_specs, check_vma=False
    )
```

profile of v0, /device:TPU:1, one launch (start us, length us, event | category | flops | bytes accessed | tf_op | source)
XLA Modules:
  0.0 48.6 jit_solution(11517302686968148341)
XLA Ops:
  0.6 2.7 %pack.1 = (f32[288,128]{1,0:T(8,128)S(1)}, f32[216,128]{1,0:T(8,128)S(1)}, f32[216,128]{1,0:T(8,128)S(1)}, f32[216,128]{1,0:T(8,128)S(1)}, f32[216,128]{1,0:T(8,...) custom-call(f32[8,2048]{1,0:T(8,128)} %refs_0_.1, ...), custom_call_target="tpu_custom_call" | custom-call | tf_op jit(solution)/shard_map/pack/pallas_call | solution.py:401
  3.3 11.1 %collective-permute-start = (f32[216,128]{1,0:T(8,128)S(1)}, f32[216,128]{1,0:T(8,128)S(1)}, u32[]{:S(2)}, u32[]{:S(2)}) collective-permute-start(f32[216,128]{1,0:T(8,128)S(1)} %get-tuple-element.37), channel_id=1, source_target_pairs={{0,254},{1,255},{2,0},{3,1},{4,2},{5,3},{6,4},{7,5},{8,6},{9,7},{1... | collective-permute-start | bytes 331784 | tf_op jit(solution)/shard_map/ppermute | solution.py:433
  14.5 1.2 %collective-permute-start.1 = (f32[216,128]{1,0:T(8,128)S(1)}, f32[216,128]{1,0:T(8,128)S(1)}, u32[]{:S(2)}, u32[]{:S(2)}) collective-permute-start(f32[216,128]{1,0:T(8,128)S(1)} %get-tuple-element.38), channel_id=1, source_target_pairs={{0,252},{1,253},{2,254},{3,255},{4,0},{5,1},{6,2},{7,3},{8,4},{9,5... | collective-permute-start | bytes 331784 | tf_op jit(solution)/shard_map/ppermute | solution.py:433
  15.6 1.2 %collective-permute-start.2 = (f32[216,128]{1,0:T(8,128)S(1)}, f32[216,128]{1,0:T(8,128)S(1)}, u32[]{:S(2)}, u32[]{:S(2)}) collective-permute-start(f32[216,128]{1,0:T(8,128)S(1)} %get-tuple-element.39), channel_id=1, source_target_pairs={{0,255},{1,0},{2,1},{3,2},{4,3},{5,4},{6,5},{7,6},{8,7},{9,8},{10,... | collective-permute-start | bytes 331784 | tf_op jit(solution)/shard_map/ppermute | solution.py:433
  16.9 0.6 %collective-permute-start.3 = (f32[216,128]{1,0:T(8,128)S(1)}, f32[216,128]{1,0:T(8,128)S(1)}, u32[]{:S(2)}, u32[]{:S(2)}) collective-permute-start(f32[216,128]{1,0:T(8,128)S(1)} %get-tuple-element.40), channel_id=1, source_target_pairs={{0,1},{1,2},{2,3},{3,4},{4,5},{5,6},{6,7},{7,8},{8,9},{9,10},{10,1... | collective-permute-start | bytes 331784 | tf_op jit(solution)/shard_map/ppermute | solution.py:433
  17.5 0.0 collective-permute-start.6
  17.5 6.6 %inner.1 = (f32[1,1024]{1,0:T(1,128)S(1)}, f32[16,128]{1,0:T(8,128)S(1)}) custom-call(bf16[768,256]{1,0:T(8,128)(2,1)S(1)} %get-tuple-element.55.tab_ref, f32[8,2048]{1,0:T(8,128)S(1)} %get-tuple-element.45.p_ref, f32[8,2048]{1,0:T(8,128)S(1)} %get-tuple-element.46.q_ref, f32[16,128]{1,0:T(8,128)S(1)} %get-tuple-element.47.k_ref, ...), custom_call_target="tpu_custom_call" | custom-call | flops 4000000000 | bytes 10000000 | tf_op jit(solution)/shard_map/inner/pallas_call | solution.py:434
  24.1 3.5 %collective-permute-done.6.refs_6_ = f32[288,128]{1,0:T(8,128)S(1)} collective-permute-done((f32[288,128]{1,0:T(8,128)S(1)}, f32[288,128]{1,0:T(8,128)S(1)}, u32[]{:S(2)}, u32[]{:S(2)}) %collective-permute-start.6) | collective-permute-done | bytes 147488 | tf_op jit(solution)/shard_map/ppermute | solution.py:429
  27.6 3.4 %collective-permute-start.4 = (f32[216,128]{1,0:T(8,128)S(1)}, f32[216,128]{1,0:T(8,128)S(1)}, u32[]{:S(2)}, u32[]{:S(2)}) collective-permute-start(f32[216,128]{1,0:T(8,128)S(1)} %get-tuple-element.41), channel_id=1, source_target_pairs={{0,4},{1,5},{2,6},{3,7},{4,8},{5,9},{6,10},{7,11},{8,12},{9,13},{1... | collective-permute-start | bytes 331784 | tf_op jit(solution)/shard_map/ppermute | solution.py:433
  31.1 0.0 collective-permute-done.refs_0_
  31.1 0.0 collective-permute-start.5
  31.1 0.0 collective-permute-done.1.refs_1_
  31.1 0.1 collective-permute-start.7
  31.2 3.7 %edge.1 = (f32[1,1536]{1,0:T(1,128)S(1)}, f32[192,512]{1,0:T(8,128)S(1)}, f32[192,512]{1,0:T(8,128)S(1)}) custom-call(bf16[768,256]{1,0:T(8,128)(2,1)S(1)} %get-tuple-element.55.tab_ref, f32[3,8,2048]{2,1,0:T(8,128)S(1)} %get-tuple-element.56.d_ref, f32[3,8,2048]{2,1,0:T(8,128)S(1)} %get-tuple-element.57.a_ref, ...), custom_call_target="tpu_custom_call" | custom-call | flops 2000000000 | bytes 10000000 | tf_op jit(solution)/shard_map/edge/pallas_call | solution.py:450
  34.8 0.0 collective-permute-done.2.refs_2_
  34.8 0.0 collective-permute-done.3.refs_3_
  34.9 6.3 %collective-permute-done.4.refs_4_ = f32[216,128]{1,0:T(8,128)S(1)} collective-permute-done((f32[216,128]{1,0:T(8,128)S(1)}, f32[216,128]{1,0:T(8,128)S(1)}, u32[]{:S(2)}, u32[]{:S(2)}) %collective-permute-start.4) | collective-permute-done | bytes 110624 | tf_op jit(solution)/shard_map/ppermute | solution.py:433
  41.2 2.6 %collective-permute-done.5.refs_5_ = f32[216,128]{1,0:T(8,128)S(1)} collective-permute-done((f32[216,128]{1,0:T(8,128)S(1)}, f32[216,128]{1,0:T(8,128)S(1)}, u32[]{:S(2)}, u32[]{:S(2)}) %collective-permute-start.5) | collective-permute-done | bytes 110624 | tf_op jit(solution)/shard_map/ppermute | solution.py:433
  43.7 2.3 %near.1 = (f32[192,512]{1,0:T(8,128)S(1)}, f32[192,512]{1,0:T(8,128)S(1)}, f32[16,128]{1,0:T(8,128)S(1)}) custom-call(f32[216,128]{1,0:T(8,128)S(1)} %collective-permute-done.refs_0_, f32[216,128]{1,0:T(8,128)S(1)} %collective-permute-done.1.refs_1_, f32[216,128]{1,0:T(8,128)S(1)} %collective-permute-done.2.refs_2_, ...), custom_call_target="tpu_custom_call" | custom-call | tf_op jit(solution)/shard_map/near/pallas_call | solution.py:458
  46.0 0.0 collective-permute-done.7.refs_7_
  46.1 2.5 %tail.1 = (f32[1,2048]{1,0:T(1,128)}, f32[16,128]{1,0:T(8,128)}) custom-call(f32[216,128]{1,0:T(8,128)S(1)} %collective-permute-done.refs_0_, f32[216,128]{1,0:T(8,128)S(1)} %collective-permute-done.1.refs_1_, f32[216,128]{1,0:T(8,128)S(1)} %collective-permute-done.2.refs_2_, f32[216,128]{1,0:T(8,128)S(1)} %collective-permute-done.3.refs_3_, ...), custom_call_target="tpu_custom_call" | custom-call | tf_op jit(solution)/shard_map/tail/pallas_call | solution.py:470
Async XLA Ops:
  3.3 27.7 %collective-permute-start = (f32[216,128]{1,0:T(8,128)S(1)}, f32[216,128]{1,0:T(8,128)S(1)}, u32[]{:S(2)}, u32[]{:S(2)}) collective-permute-start(f32[216,128]{1,0:T(8,128)S(1)} %get-tuple-element.37), channel_id=1, source_target_pairs={{0,254},{1,255},{2,0},{3,1},{4,2},{5,3},{6,4},{7,5},{8,6},{9,7},{1... | collective-permute-start | bytes 331784 | tf_op jit(solution)/shard_map/ppermute | solution.py:433
  14.5 16.6 %collective-permute-start.1 = (f32[216,128]{1,0:T(8,128)S(1)}, f32[216,128]{1,0:T(8,128)S(1)}, u32[]{:S(2)}, u32[]{:S(2)}) collective-permute-start(f32[216,128]{1,0:T(8,128)S(1)} %get-tuple-element.38), channel_id=1, source_target_pairs={{0,252},{1,253},{2,254},{3,255},{4,0},{5,1},{6,2},{7,3},{8,4},{9,5... | collective-permute-start | bytes 331784 | tf_op jit(solution)/shard_map/ppermute | solution.py:433
  15.6 19.2 %collective-permute-start.2 = (f32[216,128]{1,0:T(8,128)S(1)}, f32[216,128]{1,0:T(8,128)S(1)}, u32[]{:S(2)}, u32[]{:S(2)}) collective-permute-start(f32[216,128]{1,0:T(8,128)S(1)} %get-tuple-element.39), channel_id=1, source_target_pairs={{0,255},{1,0},{2,1},{3,2},{4,3},{5,4},{6,5},{7,6},{8,7},{9,8},{10,... | collective-permute-start | bytes 331784 | tf_op jit(solution)/shard_map/ppermute | solution.py:433
  16.9 18.0 %collective-permute-start.3 = (f32[216,128]{1,0:T(8,128)S(1)}, f32[216,128]{1,0:T(8,128)S(1)}, u32[]{:S(2)}, u32[]{:S(2)}) collective-permute-start(f32[216,128]{1,0:T(8,128)S(1)} %get-tuple-element.40), channel_id=1, source_target_pairs={{0,1},{1,2},{2,3},{3,4},{4,5},{5,6},{6,7},{7,8},{8,9},{9,10},{10,1... | collective-permute-start | bytes 331784 | tf_op jit(solution)/shard_map/ppermute | solution.py:433
  17.5 10.1 %collective-permute-start.6 = (f32[288,128]{1,0:T(8,128)S(1)}, f32[288,128]{1,0:T(8,128)S(1)}, u32[]{:S(2)}, u32[]{:S(2)}) collective-permute-start(f32[288,128]{1,0:T(8,128)S(1)} %get-tuple-element.43), channel_id=1, source_target_pairs={{0,8},{1,9},{2,10},{3,11},{4,12},{5,13},{6,14},{7,15},{8,0},{9,1},... | collective-permute-start | bytes 442376 | tf_op jit(solution)/shard_map/ppermute | solution.py:429
  27.6 13.6 %collective-permute-start.4 = (f32[216,128]{1,0:T(8,128)S(1)}, f32[216,128]{1,0:T(8,128)S(1)}, u32[]{:S(2)}, u32[]{:S(2)}) collective-permute-start(f32[216,128]{1,0:T(8,128)S(1)} %get-tuple-element.41), channel_id=1, source_target_pairs={{0,4},{1,5},{2,6},{3,7},{4,8},{5,9},{6,10},{7,11},{8,12},{9,13},{1... | collective-permute-start | bytes 331784 | tf_op jit(solution)/shard_map/ppermute | solution.py:433
  31.1 12.7 %collective-permute-start.5 = (f32[216,128]{1,0:T(8,128)S(1)}, f32[216,128]{1,0:T(8,128)S(1)}, u32[]{:S(2)}, u32[]{:S(2)}) collective-permute-start(f32[216,128]{1,0:T(8,128)S(1)} %get-tuple-element.42), channel_id=1, source_target_pairs={{0,2},{1,3},{2,4},{3,5},{4,6},{5,7},{6,8},{7,9},{8,10},{9,11},{10,... | collective-permute-start | bytes 331784 | tf_op jit(solution)/shard_map/ppermute | solution.py:433
  31.1 15.0 %collective-permute-start.7 = (f32[288,128]{1,0:T(8,128)S(1)}, f32[288,128]{1,0:T(8,128)S(1)}, u32[]{:S(2)}, u32[]{:S(2)}) collective-permute-start(f32[288,128]{1,0:T(8,128)S(1)} %collective-permute-done.6.refs_6_), channel_id=1, source_target_pairs={{0,16},{1,17},{2,18},{3,19},{4,20},{5,21},{6,22},{7,23},{8,248},{9... | collective-permute-start | bytes 442376 | tf_op jit(solution)/shard_map/ppermute | solution.py:447
where the time goes:
time: 48.7 us; the launch traced here: 48.6 us
  Pallas kernels  17.8 us (37%)
  starting transfers between devices  17.7 us (36%)
  waiting for transfers between devices  12.4 us (25%)
  between operations  0.69 us (1%)
    ppermute x6, starting transfers between devices, on_device(): near.append(lax.ppermute(packed[number + 1], 'dom', pairs))  17.6 us
    ppermute x6, waiting for transfers between devices, on_device(): near.append(lax.ppermute(packed[number + 1], 'dom', pairs))  8.89 us
    pallas_call x1, Pallas kernels, on_device(): pl.pallas_call(inner_kernel, out_shape=[shape(1, EARLY), shape(OWN_CHUNKS...  6.58 us
    pallas_call x1, Pallas kernels, on_device(): pl.pallas_call(edge_kernel, out_shape=[shape(1, OWN), shape(192, EB), sha...  3.67 us
    ppermute x1, waiting for transfers between devices, on_device(): lax.ppermute(packed[0], 'dom', [(source, source ^ 8) for source in range(...  3.53 us
    pallas_call x1, Pallas kernels, on_device(): pl.pallas_call(pack_kernel, out_shape=[shape(FAR_ROWS, LANES)] + [shape(R...  2.7 us
    pallas_call x1, Pallas kernels, on_device(): pl.pallas_call(tail_kernel, out_shape=[shape(1, EL), shape(OWN_CHUNKS, LA...  2.52 us
    pallas_call x1, Pallas kernels, on_device(): pl.pallas_call(near_kernel, out_shape=[shape(192, EB), shape(192, EB), sh...  2.31 us
  transfers between devices with their start and end apart: 8, of which 3 were waited for; matrix products, arithmetic and copies ran while one was open for 0% of the time, Pallas kernels for 26%

commit v1 on v0

--- a/solution.py
+++ b/solution.py
@@ -179,15 +179,15 @@
 
 
 def pack_kernel(*refs):
-    sources, outs, raw_s, sem = refs[:SOURCES], refs[SOURCES:-2], refs[-2], refs[-1]
+    sources, outs, (raw_s, sn_ref, sem) = refs[:SOURCES], refs[SOURCES:-3], refs[-3:]
     far_ref, near_refs, cells_ref, faces_ref = outs[0], outs[1 : NEAR + 1], outs[NEAR + 1], outs[NEAR + 2]
-    tab_ref, local = outs[NEAR + 3], outs[NEAR + 4 :]
+    tab_ref, local = outs[NEAR + 3], (*outs[NEAR + 4 :], sn_ref)
     copies = [pltpu.make_async_copy(far, near, sem.at[n]) for n, (far, near) in enumerate(zip(sources, local))]
     for copy in copies:
         copy.start()
-    for copy in copies[:8]:
+    for copy in (*copies[:4], copies[-1]):
         copy.wait()
-    p_ref, q_ref, k_ref, cf_ref, sc_ref, sn_ref, d_ref, a_ref = local[:8]
+    p_ref, q_ref, k_ref, cf_ref, sc_ref, d_ref, a_ref = local[:7]
     nodes = node_tables(d_ref, a_ref)
     cells = cell_tables(p_ref, q_ref)
     perm = [k_ref[0:8, :], k_ref[8:16, :]]
@@ -202,6 +202,8 @@
             ref[base + 16 * m + 8 : base + 16 * m + 16, :] = qa
             ref[base + 128 + m : base + 129 + m, :] = ka
             ref[base + 136 + m : base + 137 + m, :] = slot
+    for copy in copies[4:7]:
+        copy.wait()
     fill_table(raw_s, tab_ref, OWN_CHUNKS, lambda number, chunk: nodes[number](chunk))
     for j in range(SLOTS):
         out, start = (near_refs[ORDER.index(j)], 0) if j < NEAR else (far_ref, BLOCK * (j - NEAR))
@@ -216,7 +218,7 @@
             ref[base : base + 8, :] = pb
             ref[base + 8 : base + 16, :] = qb
             ref[base + 16 : base + 24, :] = kb
-    for copy in copies[8:]:
+    for copy in copies[7:-1]:
         copy.wait()
 
 
@@ -229,7 +231,10 @@
 FAR_ROWS = FAR_FACES + 144
 
 
-def inner_kernel(tab_ref, p_ref, q_ref, k_ref, y_ref, s_ref, en_ref, if_ref, gy_ref, gp_ref, f_s, a_s, t_s):
+def inner_kernel(
+    tab_ref, d_ref, a_ref, p_ref, q_ref, k_ref, y_ref, s_ref, en_ref, if_ref, gy_ref, gp_ref, fo_ref, ao_ref, f_s, a_s, t_s
+):
+    nodes = node_tables(d_ref, a_ref)
     cells = cell_tables(p_ref, q_ref)
     perm = [k_ref[0:8, :], k_ref[8:16, :]]
     width = FACE_BLOCK * LANES
@@ -260,24 +265,18 @@
     steps = FI // width
     total = lax.fori_loop(0, steps, block, jnp.zeros((16, LANES), jnp.float32))
     gp_ref[...] = add(steps - 1, total)
-    gy_ref[...] = -y_ref[:, :EARLY] * strain_of(s_ref, f_s, a_s)
-
-
-def edge_kernel(tab_ref, d_ref, a_ref, y_ref, s_ref, en_ref, gyi_ref, gy_ref, fo_ref, ao_ref, f_s, a_s):
-    nodes = node_tables(d_ref, a_ref)
-
-    def block(step, _):
+
+    def late(step, _):
         start = pl.multiple_of(step * LANES, LANES)
-        cols = pl.ds(start, LANES)
-        elem = en_ref[:, pl.ds(pl.multiple_of(EARLY + start, LANES), LANES)]
-        own_corners(tab_ref, nodes, elem, ((0, 1), (2, 3), (4, 5)), (6, 7), f_s, a_s, cols)
+        place = pl.multiple_of(EARLY + start, LANES)
+        elem = en_ref[:, pl.ds(place, LANES)]
+        own_corners(tab_ref, nodes, elem, ((0, 1), (2, 3), (4, 5)), (6, 7), f_s, a_s, pl.ds(place, LANES))
         elem = en_ref[:, pl.ds(pl.multiple_of(OWN + start, LANES), LANES)]
-        own_corners(tab_ref, nodes, elem, ((1, 2), (3, 4)), (5, 6, 7), fo_ref, ao_ref, cols)
+        own_corners(tab_ref, nodes, elem, ((1, 2), (3, 4)), (5, 6, 7), fo_ref, ao_ref, pl.ds(start, LANES))
         return 0
 
-    lax.fori_loop(0, EB // LANES, block, 0)
-    gy_ref[:, :EARLY] = gyi_ref[...]
-    gy_ref[:, EARLY:] = -y_ref[:, EARLY:OWN] * strain_of(s_ref, f_s, a_s)
+    lax.fori_loop(0, EB // LANES, late, 0)
+    gy_ref[...] = -y_ref[:, :OWN] * strain_of(s_ref, f_s, a_s)
 
 
 def incoming(got, cells_ref, sc_ref, slots, i_s, t_s, start):
@@ -308,19 +307,6 @@
     return lax.fori_loop(0, count, add, total)
 
 
-def near_kernel(*refs):
-    near, (fo_ref, ao_ref, cells_ref, sc_ref, en_ref, gpi_ref) = refs[:NEAR], refs[NEAR : NEAR + 6]
-    f_ref, a_ref, gp_ref, i_s, t_s, raw_s, tab_s = refs[NEAR + 6 :]
-    got = [near[ORDER.index(j)] for j in range(NEAR)]
-    fill_table(raw_s, tab_s, NEAR, lambda number, chunk: got[chunk][8 * number : 8 * number + 8, :])
-    for step in range(EB // LANES):
-        elem = en_ref[:, OWN + step * LANES : OWN + (step + 1) * LANES]
-        cols = slice(step * LANES, (step + 1) * LANES)
-        ghost_corners(tab_s, elem, OWN_CHUNKS, OWN_CHUNKS + NEAR, fo_ref, ao_ref, f_ref, a_ref, cols, True)
-    incoming(got, cells_ref, sc_ref, range(NEAR), i_s, t_s, 0)
-    gp_ref[...] = add_terms(i_s, t_s, NEAR, gpi_ref[...])
-
-
 def tail_kernel(*refs):
     near, (swapped, relayed) = refs[:NEAR], refs[NEAR : NEAR + 2]
     (fo_ref, ao_ref, cells_ref, faces_ref, y_ref, s_ref, sc_ref, en_ref, cf_ref, gyi_ref, gpi_ref) = refs[NEAR + 2 : NEAR + 13]
@@ -333,13 +319,11 @@
                 ref[to + row : to + row + 8, :] = jnp.where(
                     low, direct[source + row : source + row + 8, :], other[source + row : source + row + 8, :]
                 )
-    fill_table(raw_s, tab_s, 2, lambda number, chunk: got[NEAR + chunk][8 * number : 8 * number + 8, :])
+    fill_table(raw_s, tab_s, SLOTS, lambda number, chunk: got[chunk][8 * number : 8 * number + 8, :])
     for step in range(EB // LANES):
         elem = en_ref[:, OWN + step * LANES : OWN + (step + 1) * LANES]
         cols = slice(step * LANES, (step + 1) * LANES)
-        ghost_corners(
-            tab_s, elem, OWN_CHUNKS + NEAR, OWN_CHUNKS + SLOTS, fo_ref, ao_ref, f_s, a_s, cols, False
-        )
+        ghost_corners(tab_s, elem, OWN_CHUNKS, OWN_CHUNKS + SLOTS, fo_ref, ao_ref, f_s, a_s, cols, True)
 
     ghosts = [
         lambda h: got[h][NODE_ROWS : NODE_ROWS + 8, :],
@@ -356,8 +340,8 @@
         ka = faces_ref[128 + m : 129 + m, :]
         i_s[0:1, cols] = cf_ref[0:1, cols]
         t_s[0:1, cols] = face_terms(pa, qa, ka, pb, qb, kb)[0]
-    incoming(got, cells_ref, sc_ref, (6, 7), i_s, t_s, FX)
-    gp_ref[...] = add_terms(i_s, t_s, 3, gpi_ref[...])
+    incoming(got, cells_ref, sc_ref, range(SLOTS), i_s, t_s, FX)
+    gp_ref[...] = add_terms(i_s, t_s, SLOTS + 1, gpi_ref[...])
     gy_ref[:, :OWN] = gyi_ref[...]
     gy_ref[:, OWN:] = -y_ref[:, OWN:] * strain_of(s_ref, f_s, a_s)
 
@@ -390,13 +374,13 @@
         perm,
         cross_faces,
         send_cells,
-        send_nodes,
         forward,
         adjoint,
         elem_nodes,
         inner_faces,
         young,
         stiffness,
+        send_nodes,
     )
     packed = pl.pallas_call(
         pack_kernel,
@@ -404,9 +388,13 @@
         + [shape(ROWS, LANES)] * NEAR
         + [shape(24 * SLOTS, LANES), shape(144, LANES)]
         + [jax.ShapeDtypeStruct((48 * OWN_CHUNKS, 2 * LANES), jnp.bfloat16)]
-        + [jax.ShapeDtypeStruct(one.shape, one.dtype) for one in sources],
+        + [jax.ShapeDtypeStruct(one.shape, one.dtype) for one in sources[:-1]],
         in_specs=[pl.BlockSpec(memory_space=pltpu.HBM)] * SOURCES,
-        scratch_shapes=[pltpu.VMEM((48 * OWN_CHUNKS, LANES), jnp.float32), pltpu.SemaphoreType.DMA((SOURCES,))],
+        scratch_shapes=[
+            pltpu.VMEM((48 * OWN_CHUNKS, LANES), jnp.float32),
+            pltpu.VMEM((SLOTS, LANES), jnp.int32),
+            pltpu.SemaphoreType.DMA((SOURCES,)),
+        ],
         compiler_params=VMEM,
         name="pack",
     )(*(pltpu.with_memory_space_constraint(one, pltpu.HBM) for one in sources))
@@ -417,7 +405,6 @@
         perm,
         cross_faces,
         send_cells,
-        _,
         forward,
         adjoint,
         elem_nodes,
@@ -431,52 +418,31 @@
     for number, j in enumerate(ORDER):
         pairs = [(source, (source - OFFSETS[j]) % count) for source in range(count)]
         near.append(lax.ppermute(packed[number + 1], "dom", pairs))
-    inner_young, inner_perm = pl.pallas_call(
+    relayed = lax.ppermute(
+        swapped, "dom", [(source, (source - 16 if source & 8 else source + 16) % count) for source in range(count)]
+    )
+    own_young, own_perm, edge_forward, edge_adjoint = pl.pallas_call(
         inner_kernel,
-        out_shape=[shape(1, EARLY), shape(OWN_CHUNKS, LANES)],
+        out_shape=[shape(1, OWN), shape(OWN_CHUNKS, LANES), shape(192, EB), shape(192, EB)],
         scratch_shapes=[
-            pltpu.VMEM((192, EARLY), jnp.float32),
-            pltpu.VMEM((192, EARLY), jnp.float32),
+            pltpu.VMEM((192, OWN), jnp.float32),
+            pltpu.VMEM((192, OWN), jnp.float32),
             pltpu.VMEM((2, FI), jnp.float32),
         ],
         compiler_params=VMEM,
         cost_estimate=pl.CostEstimate(flops=4 * 10**9, bytes_accessed=10**7, transcendentals=0),
         name="inner",
-    )(table, pressure, adjoint_pressure, perm, young, stiffness, elem_nodes, inner_faces)
-    swapped, inner_young, inner_perm, table = lax.optimization_barrier((swapped, inner_young, inner_perm, table))
-    relayed = lax.ppermute(
-        swapped, "dom", [(source, (source - 16 if source & 8 else source + 16) % count) for source in range(count)]
-    )
-    own_young, edge_forward, edge_adjoint = pl.pallas_call(
-        edge_kernel,
-        out_shape=[shape(1, OWN), shape(192, EB), shape(192, EB)],
-        scratch_shapes=[pltpu.VMEM((192, EB), jnp.float32), pltpu.VMEM((192, EB), jnp.float32)],
-        compiler_params=VMEM,
-        cost_estimate=pl.CostEstimate(flops=2 * 10**9, bytes_accessed=10**7, transcendentals=0),
-        name="edge",
-    )(table, forward, adjoint, young, stiffness, elem_nodes, inner_young)
-    edge_forward, edge_adjoint, near_perm = pl.pallas_call(
-        near_kernel,
-        out_shape=[shape(192, EB), shape(192, EB), shape(OWN_CHUNKS, LANES)],
-        scratch_shapes=[
-            pltpu.VMEM((1, NEAR * FX), jnp.int32),
-            pltpu.VMEM((1, NEAR * FX), jnp.float32),
-            pltpu.VMEM((48 * NEAR, LANES), jnp.float32),
-            pltpu.VMEM((48 * NEAR, 2 * LANES), jnp.bfloat16),
-        ],
-        compiler_params=VMEM,
-        name="near",
-    )(*near, edge_forward, edge_adjoint, cells, send_cells, elem_nodes, inner_perm)
+    )(table, forward, adjoint, pressure, adjoint_pressure, perm, young, stiffness, elem_nodes, inner_faces)
     grad_young, grad_perm = pl.pallas_call(
         tail_kernel,
         out_shape=[shape(1, EL), shape(OWN_CHUNKS, LANES)],
         scratch_shapes=[
             pltpu.VMEM((192, EB), jnp.float32),
             pltpu.VMEM((192, EB), jnp.float32),
-            pltpu.VMEM((1, 3 * FX), jnp.int32),
-            pltpu.VMEM((1, 3 * FX), jnp.float32),
-            pltpu.VMEM((96, LANES), jnp.float32),
-            pltpu.VMEM((96, 2 * LANES), jnp.bfloat16),
+            pltpu.VMEM((1, (SLOTS + 1) * FX), jnp.int32),
+            pltpu.VMEM((1, (SLOTS + 1) * FX), jnp.float32),
+            pltpu.VMEM((48 * SLOTS, LANES), jnp.float32),
+            pltpu.VMEM((48 * SLOTS, 2 * LANES), jnp.bfloat16),
             pltpu.VMEM((ROWS, LANES), jnp.float32),
             pltpu.VMEM((ROWS, LANES), jnp.float32),
         ],
@@ -496,7 +462,7 @@
         elem_nodes,
         cross_faces,
         own_young,
-        near_perm,
+        own_perm,
     )
     return (grad_young.reshape(EL), grad_perm.reshape(EL))
 

time: 48.7 us -> 42.2 us (0.87)
  waiting for transfers between devices: 12.4 us -> 8.29 us
  Pallas kernels: 17.8 us -> 16.3 us
  starting transfers between devices: 17.7 us -> 16.8 us
    ppermute x6, starting transfers between devices: 17.6 us -> 7.74 us  [on_device(): near.append(lax.ppermute(packed[number + 1], 'dom', pairs))]
    ppermute x1, starting transfers between devices: 0.01 us -> 7.81 us  [on_device(): lax.ppermute(packed[0], 'dom', [(source, source ^ 8) for source in range(...]
    ppermute x1, waiting for transfers between devices: 3.53 us -> 0.01 us  [on_device(): lax.ppermute(packed[0], 'dom', [(source, source ^ 8) for source in range(...]
    pallas_call x3 -> x1, Pallas kernels: 12.6 us -> 9.83 us  [on_device(): pl.pallas_call(inner_kernel, out_shape=[shape(1, OWN), shape(OWN_CHUNKS,...]
    pallas_call x1, Pallas kernels: 2.52 us -> 4.33 us  [on_device(): pl.pallas_call(tail_kernel, out_shape=[shape(1, EL), shape(OWN_CHUNKS, LA...]
    ppermute x6, waiting for transfers between devices: 8.89 us -> 7.31 us  [on_device(): near.append(lax.ppermute(packed[number + 1], 'dom', pairs))]
    ppermute x1, starting transfers between devices: 0.08 us -> 1.22 us  [on_device(): lax.ppermute(swapped, 'dom', [(source, (source - 16 if source & 8 else so...]
    ppermute x1, waiting for transfers between devices: 0.01 us -> 0.98 us  [on_device(): lax.ppermute(swapped, 'dom', [(source, (source - 16 if source & 8 else so...]
  transfers between devices with their start and end apart: 8 -> 8, of which waited for: 3 -> 3; matrix products, arithmetic and copies ran while one was open for 0% -> 0% of each run, Pallas kernels for 26% -> 23%
where the time goes in v1:
time: 42.2 us; the launch traced here: 42.1 us
  starting transfers between devices  16.8 us (40%)
  Pallas kernels  16.3 us (39%)
  waiting for transfers between devices  8.29 us (20%)
  between operations  0.69 us (2%)
    pallas_call x1, Pallas kernels, on_device(): pl.pallas_call(inner_kernel, out_shape=[shape(1, OWN), shape(OWN_CHUNKS,...  9.83 us
    ppermute x1, starting transfers between devices, on_device(): lax.ppermute(packed[0], 'dom', [(source, source ^ 8) for source in range(...  7.81 us
    ppermute x6, starting transfers between devices, on_device(): near.append(lax.ppermute(packed[number + 1], 'dom', pairs))  7.74 us
    ppermute x6, waiting for transfers between devices, on_device(): near.append(lax.ppermute(packed[number + 1], 'dom', pairs))  7.31 us
    pallas_call x1, Pallas kernels, on_device(): pl.pallas_call(tail_kernel, out_shape=[shape(1, EL), shape(OWN_CHUNKS, LA...  4.33 us
    pallas_call x1, Pallas kernels, on_device(): pl.pallas_call(pack_kernel, out_shape=[shape(FAR_ROWS, LANES)] + [shape(R...  2.19 us
    ppermute x1, starting transfers between devices, on_device(): lax.ppermute(swapped, 'dom', [(source, (source - 16 if source & 8 else so...  1.22 us
    ppermute x1, waiting for transfers between devices, on_device(): lax.ppermute(swapped, 'dom', [(source, (source - 16 if source & 8 else so...  0.98 us
  transfers between devices with their start and end apart: 8, of which 3 were waited for; matrix products, arithmetic and copies ran while one was open for 0% of the time, Pallas kernels for 23%

profile of v1, /device:TPU:1, one launch (start us, length us, event | category | flops | bytes accessed | tf_op | source)
XLA Modules:
  0.0 42.1 jit_solution(12185760965093990381)
XLA Ops:
  0.6 2.2 %pack.1 = (f32[288,128]{1,0:T(8,128)S(1)}, f32[216,128]{1,0:T(8,128)S(1)}, f32[216,128]{1,0:T(8,128)S(1)}, f32[216,128]{1,0:T(8,128)S(1)}, f32[216,128]{1,0:T(8,...) custom-call(f32[8,2048]{1,0:T(8,128)} %refs_0_.1, ...), custom_call_target="tpu_custom_call" | custom-call | tf_op jit(solution)/shard_map/pack/pallas_call | solution.py:385
  2.8 7.8 %collective-permute-start.6 = (f32[288,128]{1,0:T(8,128)S(1)}, f32[288,128]{1,0:T(8,128)S(1)}, u32[]{:S(2)}, u32[]{:S(2)}) collective-permute-start(f32[288,128]{1,0:T(8,128)S(1)} %get-tuple-element.35), channel_id=1, source_target_pairs={{0,8},{1,9},{2,10},{3,11},{4,12},{5,13},{6,14},{7,15},{8,0},{9,1},... | collective-permute-start | bytes 442376 | tf_op jit(solution)/shard_map/ppermute | solution.py:416
  10.6 4.5 %collective-permute-start = (f32[216,128]{1,0:T(8,128)S(1)}, f32[216,128]{1,0:T(8,128)S(1)}, u32[]{:S(2)}, u32[]{:S(2)}) collective-permute-start(f32[216,128]{1,0:T(8,128)S(1)} %get-tuple-element.29), channel_id=1, source_target_pairs={{0,254},{1,255},{2,0},{3,1},{4,2},{5,3},{6,4},{7,5},{8,6},{9,7},{1... | collective-permute-start | bytes 331784 | tf_op jit(solution)/shard_map/ppermute | solution.py:420
  15.1 0.1 collective-permute-start.1
  15.2 1.2 %collective-permute-start.2 = (f32[216,128]{1,0:T(8,128)S(1)}, f32[216,128]{1,0:T(8,128)S(1)}, u32[]{:S(2)}, u32[]{:S(2)}) collective-permute-start(f32[216,128]{1,0:T(8,128)S(1)} %get-tuple-element.31), channel_id=1, source_target_pairs={{0,255},{1,0},{2,1},{3,2},{4,3},{5,4},{6,5},{7,6},{8,7},{9,8},{10,... | collective-permute-start | bytes 331784 | tf_op jit(solution)/shard_map/ppermute | solution.py:420
  16.5 1.1 %collective-permute-start.3 = (f32[216,128]{1,0:T(8,128)S(1)}, f32[216,128]{1,0:T(8,128)S(1)}, u32[]{:S(2)}, u32[]{:S(2)}) collective-permute-start(f32[216,128]{1,0:T(8,128)S(1)} %get-tuple-element.32), channel_id=1, source_target_pairs={{0,1},{1,2},{2,3},{3,4},{4,5},{5,6},{6,7},{7,8},{8,9},{9,10},{10,1... | collective-permute-start | bytes 331784 | tf_op jit(solution)/shard_map/ppermute | solution.py:420
  17.5 2.9 %collective-permute-done.refs_0_ = f32[216,128]{1,0:T(8,128)S(1)} collective-permute-done((f32[216,128]{1,0:T(8,128)S(1)}, f32[216,128]{1,0:T(8,128)S(1)}, u32[]{:S(2)}, u32[]{:S(2)}) %collective-permute-start) | collective-permute-done | bytes 110624 | tf_op jit(solution)/shard_map/ppermute | solution.py:420
  20.4 0.8 %collective-permute-start.4 = (f32[216,128]{1,0:T(8,128)S(1)}, f32[216,128]{1,0:T(8,128)S(1)}, u32[]{:S(2)}, u32[]{:S(2)}) collective-permute-start(f32[216,128]{1,0:T(8,128)S(1)} %get-tuple-element.33), channel_id=1, source_target_pairs={{0,4},{1,5},{2,6},{3,7},{4,8},{5,9},{6,10},{7,11},{8,12},{9,13},{1... | collective-permute-start | bytes 331784 | tf_op jit(solution)/shard_map/ppermute | solution.py:420
  21.2 4.4 %collective-permute-done.1.refs_1_ = f32[216,128]{1,0:T(8,128)S(1)} collective-permute-done((f32[216,128]{1,0:T(8,128)S(1)}, f32[216,128]{1,0:T(8,128)S(1)}, u32[]{:S(2)}, u32[]{:S(2)}) %collective-permute-start.1) | collective-permute-done | bytes 110624 | tf_op jit(solution)/shard_map/ppermute | solution.py:420
  25.7 0.0 collective-permute-start.5
  25.7 0.0 collective-permute-done.6.refs_6_
  25.7 1.2 %collective-permute-start.7 = (f32[288,128]{1,0:T(8,128)S(1)}, f32[288,128]{1,0:T(8,128)S(1)}, u32[]{:S(2)}, u32[]{:S(2)}) collective-permute-start(f32[288,128]{1,0:T(8,128)S(1)} %collective-permute-done.6.refs_6_), channel_id=1, source_target_pairs={{0,16},{1,17},{2,18},{3,19},{4,20},{5,21},{6,22},{7,23},{8,248},{9... | collective-permute-start | bytes 442376 | tf_op jit(solution)/shard_map/ppermute | solution.py:421
  26.9 9.8 %inner.1 = (f32[1,1536]{1,0:T(1,128)S(1)}, f32[16,128]{1,0:T(8,128)S(1)}, f32[192,512]{1,0:T(8,128)S(1)}, f32[192,512]{1,0:T(8,128)S(1)}) custom-call(bf16[768,256]{1,0:T(8,128)(2,1)S(1)} %get-tuple-element.36.tab_ref, f32[3,8,2048]{2,1,0:T(8,128)S(1)} %get-tuple-element.37.d_ref, f32[3,8,2048]{2,1,0:T(8,128)S(1)} %get-tuple-element.38.a_ref, ...), custom_call_target="tpu_custom_call" | custom-call | flops 4000000000 | bytes 10000000 | tf_op jit(solution)/shard_map/inner/pallas_call | solution.py:424
  36.7 0.0 collective-permute-done.2.refs_2_
  36.7 0.0 collective-permute-done.3.refs_3_
  36.8 0.0 collective-permute-done.4.refs_4_
  36.8 0.0 collective-permute-done.5.refs_5_
  36.8 1.0 %collective-permute-done.7.refs_7_ = f32[288,128]{1,0:T(8,128)S(1)} collective-permute-done((f32[288,128]{1,0:T(8,128)S(1)}, f32[288,128]{1,0:T(8,128)S(1)}, u32[]{:S(2)}, u32[]{:S(2)}) %collective-permute-start.7) | collective-permute-done | bytes 147488 | tf_op jit(solution)/shard_map/ppermute | solution.py:421
  37.8 4.3 %tail.1 = (f32[1,2048]{1,0:T(1,128)}, f32[16,128]{1,0:T(8,128)}) custom-call(f32[216,128]{1,0:T(8,128)S(1)} %collective-permute-done.refs_0_, f32[216,128]{1,0:T(8,128)S(1)} %collective-permute-done.1.refs_1_, f32[216,128]{1,0:T(8,128)S(1)} %collective-permute-done.2.refs_2_, f32[216,128]{1,0:T(8,128)S(1)} %collective-permute-done.3.refs_3_, ...), custom_call_target="tpu_custom_call" | custom-call | tf_op jit(solution)/shard_map/tail/pallas_call | solution.py:436
Async XLA Ops:
  2.8 22.9 %collective-permute-start.6 = (f32[288,128]{1,0:T(8,128)S(1)}, f32[288,128]{1,0:T(8,128)S(1)}, u32[]{:S(2)}, u32[]{:S(2)}) collective-permute-start(f32[288,128]{1,0:T(8,128)S(1)} %get-tuple-element.35), channel_id=1, source_target_pairs={{0,8},{1,9},{2,10},{3,11},{4,12},{5,13},{6,14},{7,15},{8,0},{9,1},... | collective-permute-start | bytes 442376 | tf_op jit(solution)/shard_map/ppermute | solution.py:416
  10.6 9.8 %collective-permute-start = (f32[216,128]{1,0:T(8,128)S(1)}, f32[216,128]{1,0:T(8,128)S(1)}, u32[]{:S(2)}, u32[]{:S(2)}) collective-permute-start(f32[216,128]{1,0:T(8,128)S(1)} %get-tuple-element.29), channel_id=1, source_target_pairs={{0,254},{1,255},{2,0},{3,1},{4,2},{5,3},{6,4},{7,5},{8,6},{9,7},{1... | collective-permute-start | bytes 331784 | tf_op jit(solution)/shard_map/ppermute | solution.py:420
  15.1 10.6 %collective-permute-start.1 = (f32[216,128]{1,0:T(8,128)S(1)}, f32[216,128]{1,0:T(8,128)S(1)}, u32[]{:S(2)}, u32[]{:S(2)}) collective-permute-start(f32[216,128]{1,0:T(8,128)S(1)} %get-tuple-element.30), channel_id=1, source_target_pairs={{0,252},{1,253},{2,254},{3,255},{4,0},{5,1},{6,2},{7,3},{8,4},{9,5... | collective-permute-start | bytes 331784 | tf_op jit(solution)/shard_map/ppermute | solution.py:420
  15.2 21.5 %collective-permute-start.2 = (f32[216,128]{1,0:T(8,128)S(1)}, f32[216,128]{1,0:T(8,128)S(1)}, u32[]{:S(2)}, u32[]{:S(2)}) collective-permute-start(f32[216,128]{1,0:T(8,128)S(1)} %get-tuple-element.31), channel_id=1, source_target_pairs={{0,255},{1,0},{2,1},{3,2},{4,3},{5,4},{6,5},{7,6},{8,7},{9,8},{10,... | collective-permute-start | bytes 331784 | tf_op jit(solution)/shard_map/ppermute | solution.py:420
  16.5 20.3 %collective-permute-start.3 = (f32[216,128]{1,0:T(8,128)S(1)}, f32[216,128]{1,0:T(8,128)S(1)}, u32[]{:S(2)}, u32[]{:S(2)}) collective-permute-start(f32[216,128]{1,0:T(8,128)S(1)} %get-tuple-element.32), channel_id=1, source_target_pairs={{0,1},{1,2},{2,3},{3,4},{4,5},{5,6},{6,7},{7,8},{8,9},{9,10},{10,1... | collective-permute-start | bytes 331784 | tf_op jit(solution)/shard_map/ppermute | solution.py:420
  20.4 16.4 %collective-permute-start.4 = (f32[216,128]{1,0:T(8,128)S(1)}, f32[216,128]{1,0:T(8,128)S(1)}, u32[]{:S(2)}, u32[]{:S(2)}) collective-permute-start(f32[216,128]{1,0:T(8,128)S(1)} %get-tuple-element.33), channel_id=1, source_target_pairs={{0,4},{1,5},{2,6},{3,7},{4,8},{5,9},{6,10},{7,11},{8,12},{9,13},{1... | collective-permute-start | bytes 331784 | tf_op jit(solution)/shard_map/ppermute | solution.py:420
  25.7 11.1 %collective-permute-start.5 = (f32[216,128]{1,0:T(8,128)S(1)}, f32[216,128]{1,0:T(8,128)S(1)}, u32[]{:S(2)}, u32[]{:S(2)}) collective-permute-start(f32[216,128]{1,0:T(8,128)S(1)} %get-tuple-element.34), channel_id=1, source_target_pairs={{0,2},{1,3},{2,4},{3,5},{4,6},{5,7},{6,8},{7,9},{8,10},{9,11},{10,... | collective-permute-start | bytes 331784 | tf_op jit(solution)/shard_map/ppermute | solution.py:420
  25.7 12.1 %collective-permute-start.7 = (f32[288,128]{1,0:T(8,128)S(1)}, f32[288,128]{1,0:T(8,128)S(1)}, u32[]{:S(2)}, u32[]{:S(2)}) collective-permute-start(f32[288,128]{1,0:T(8,128)S(1)} %collective-permute-done.6.refs_6_), channel_id=1, source_target_pairs={{0,16},{1,17},{2,18},{3,19},{4,20},{5,21},{6,22},{7,23},{8,248},{9... | collective-permute-start | bytes 442376 | tf_op jit(solution)/shard_map/ppermute | solution.py:421

commit v2 on v1

--- a/solution.py
+++ b/solution.py
@@ -71,11 +71,17 @@
     return common * kb, common * ka
 
 
+def one_hot(lo):
+    rows = lax.broadcasted_iota(jnp.int32, (LANES, lo.shape[1]), 0).astype(jnp.float32).astype(jnp.bfloat16)
+    here = rows == lo.astype(jnp.float32).astype(jnp.bfloat16)
+    return jnp.where(here, jnp.bfloat16(1), jnp.bfloat16(0))
+
+
 def scatter(index, term):
     length = index.shape[1]
     lo = index & (LANES - 1)
     hi = index >> 7
-    hot = jnp.where(lax.broadcasted_iota(jnp.int32, (LANES, length), 0) == lo, 1.0, 0.0).astype(jnp.bfloat16)
+    hot = one_hot(lo)
     top = term.astype(jnp.bfloat16).astype(jnp.float32)
     rows = lax.broadcasted_iota(jnp.int32, (16, length), 0) == hi
     left = jnp.concatenate([jnp.where(rows, top, 0.0), jnp.where(rows, term - top, 0.0)], axis=0)
@@ -125,10 +131,7 @@
 
 
 def lookup(tab_ref, rows, first, last, olds=(None, None)):
-    sub = lax.broadcasted_iota(jnp.int32, (LANES, LANES), 0)
-    hot = jnp.concatenate(
-        [jnp.where(sub == (row & (LANES - 1)), 1.0, 0.0).astype(jnp.bfloat16) for row in rows], axis=1
-    )
+    hot = jnp.concatenate([one_hot(row & (LANES - 1)) for row in rows], axis=1)
     found = jnp.dot(tab_ref[...], jnp.concatenate([hot, hot], axis=0), preferred_element_type=jnp.float32)
     results = []
     for place, (row, old) in enumerate(zip(rows, olds)):
@@ -224,7 +227,7 @@
 
 FACE_BLOCK = 6
 EARLY = FI // FACE_BLOCK
-ORDER = (2, 4, 0, 1, 5, 3)
+ORDER = (3, 5, 1, 0, 4, 2)
 NEAR = len(ORDER)
 BLOCK = NODE_ROWS + 24
 FAR_FACES = 2 * BLOCK

time: 42.2 us -> 44.2 us (1.047)
  waiting for transfers between devices: 8.29 us -> 12.3 us
  starting transfers between devices: 16.8 us -> 15.1 us
    ppermute x6, waiting for transfers between devices: 7.31 us -> 12.3 us  [on_device(): near.append(lax.ppermute(packed[number + 1], 'dom', pairs))]
    ppermute x1, starting transfers between devices: 1.22 us -> 0.01 us  [on_device(): lax.ppermute(swapped, 'dom', [(source, (source - 16 if source & 8 else so...]
    ppermute x1, waiting for transfers between devices: 0.98 us -> 0.01 us  [on_device(): lax.ppermute(swapped, 'dom', [(source, (source - 16 if source & 8 else so...]
    ppermute x6, starting transfers between devices: 7.74 us -> 7.24 us  [on_device(): near.append(lax.ppermute(packed[number + 1], 'dom', pairs))]
  transfers between devices with their start and end apart: 8 -> 8, of which waited for: 3 -> 2; matrix products, arithmetic and copies ran while one was open for 0% -> 0% of each run, Pallas kernels for 23% -> 22%
where the time goes in v2:
time: 44.2 us; the launch traced here: 44.1 us
  Pallas kernels  16 us (36%)
  starting transfers between devices  15.1 us (34%)
  waiting for transfers between devices  12.3 us (28%)
  between operations  0.69 us (2%)
    ppermute x6, waiting for transfers between devices, on_device(): near.append(lax.ppermute(packed[number + 1], 'dom', pairs))  12.3 us
    pallas_call x1, Pallas kernels, on_device(): pl.pallas_call(inner_kernel, out_shape=[shape(1, OWN), shape(OWN_CHUNKS,...  9.78 us
    ppermute x1, starting transfers between devices, on_device(): lax.ppermute(packed[0], 'dom', [(source, source ^ 8) for source in range(...  7.81 us
    ppermute x6, starting transfers between devices, on_device(): near.append(lax.ppermute(packed[number + 1], 'dom', pairs))  7.24 us
    pallas_call x1, Pallas kernels, on_device(): pl.pallas_call(tail_kernel, out_shape=[shape(1, EL), shape(OWN_CHUNKS, LA...  4.08 us
    pallas_call x1, Pallas kernels, on_device(): pl.pallas_call(pack_kernel, out_shape=[shape(FAR_ROWS, LANES)] + [shape(R...  2.15 us
  transfers between devices with their start and end apart: 8, of which 2 were waited for; matrix products, arithmetic and copies ran while one was open for 0% of the time, Pallas kernels for 22%

profile of v2, /device:TPU:1, one launch (start us, length us, event | category | flops | bytes accessed | tf_op | source)
XLA Modules:
  0.0 44.1 jit_solution(3717594149683372491)
XLA Ops:
  0.6 2.2 %pack.1 = (f32[288,128]{1,0:T(8,128)S(1)}, f32[216,128]{1,0:T(8,128)S(1)}, f32[216,128]{1,0:T(8,128)S(1)}, f32[216,128]{1,0:T(8,128)S(1)}, f32[216,128]{1,0:T(8,...) custom-call(f32[8,2048]{1,0:T(8,128)} %refs_0_.1, ...), custom_call_target="tpu_custom_call" | custom-call | tf_op jit(solution)/shard_map/pack/pallas_call | solution.py:388
  2.8 7.8 %collective-permute-start.6 = (f32[288,128]{1,0:T(8,128)S(1)}, f32[288,128]{1,0:T(8,128)S(1)}, u32[]{:S(2)}, u32[]{:S(2)}) collective-permute-start(f32[288,128]{1,0:T(8,128)S(1)} %get-tuple-element.35), channel_id=1, source_target_pairs={{0,8},{1,9},{2,10},{3,11},{4,12},{5,13},{6,14},{7,15},{8,0},{9,1},... | collective-permute-start | bytes 442376 | tf_op jit(solution)/shard_map/ppermute | solution.py:419
  10.6 0.7 %collective-permute-start = (f32[216,128]{1,0:T(8,128)S(1)}, f32[216,128]{1,0:T(8,128)S(1)}, u32[]{:S(2)}, u32[]{:S(2)}) collective-permute-start(f32[216,128]{1,0:T(8,128)S(1)} %get-tuple-element.29), channel_id=1, source_target_pairs={{0,2},{1,3},{2,4},{3,5},{4,6},{5,7},{6,8},{7,9},{8,10},{9,11},{10,... | collective-permute-start | bytes 331784 | tf_op jit(solution)/shard_map/ppermute | solution.py:423
  11.3 1.2 %collective-permute-start.1 = (f32[216,128]{1,0:T(8,128)S(1)}, f32[216,128]{1,0:T(8,128)S(1)}, u32[]{:S(2)}, u32[]{:S(2)}) collective-permute-start(f32[216,128]{1,0:T(8,128)S(1)} %get-tuple-element.30), channel_id=1, source_target_pairs={{0,4},{1,5},{2,6},{3,7},{4,8},{5,9},{6,10},{7,11},{8,12},{9,13},{1... | collective-permute-start | bytes 331784 | tf_op jit(solution)/shard_map/ppermute | solution.py:423
  12.5 1.1 %collective-permute-start.2 = (f32[216,128]{1,0:T(8,128)S(1)}, f32[216,128]{1,0:T(8,128)S(1)}, u32[]{:S(2)}, u32[]{:S(2)}) collective-permute-start(f32[216,128]{1,0:T(8,128)S(1)} %get-tuple-element.31), channel_id=1, source_target_pairs={{0,1},{1,2},{2,3},{3,4},{4,5},{5,6},{6,7},{7,8},{8,9},{9,10},{10,1... | collective-permute-start | bytes 331784 | tf_op jit(solution)/shard_map/ppermute | solution.py:423
  13.7 0.4 collective-permute-start.3
  14.1 10.9 %collective-permute-done.refs_0_ = f32[216,128]{1,0:T(8,128)S(1)} collective-permute-done((f32[216,128]{1,0:T(8,128)S(1)}, f32[216,128]{1,0:T(8,128)S(1)}, u32[]{:S(2)}, u32[]{:S(2)}) %collective-permute-start) | collective-permute-done | bytes 110624 | tf_op jit(solution)/shard_map/ppermute | solution.py:423
  25.0 0.0 collective-permute-start.4
  25.0 1.4 %collective-permute-done.1.refs_1_ = f32[216,128]{1,0:T(8,128)S(1)} collective-permute-done((f32[216,128]{1,0:T(8,128)S(1)}, f32[216,128]{1,0:T(8,128)S(1)}, u32[]{:S(2)}, u32[]{:S(2)}) %collective-permute-start.1) | collective-permute-done | bytes 110624 | tf_op jit(solution)/shard_map/ppermute | solution.py:423
  26.4 3.8 %collective-permute-start.5 = (f32[216,128]{1,0:T(8,128)S(1)}, f32[216,128]{1,0:T(8,128)S(1)}, u32[]{:S(2)}, u32[]{:S(2)}) collective-permute-start(f32[216,128]{1,0:T(8,128)S(1)} %get-tuple-element.34), channel_id=1, source_target_pairs={{0,254},{1,255},{2,0},{3,1},{4,2},{5,3},{6,4},{7,5},{8,6},{9,7},{1... | collective-permute-start | bytes 331784 | tf_op jit(solution)/shard_map/ppermute | solution.py:423
  30.1 0.0 collective-permute-done.6.refs_6_
  30.2 0.0 collective-permute-start.7
  30.2 9.8 %inner.1 = (f32[1,1536]{1,0:T(1,128)S(1)}, f32[16,128]{1,0:T(8,128)S(1)}, f32[192,512]{1,0:T(8,128)S(1)}, f32[192,512]{1,0:T(8,128)S(1)}) custom-call(bf16[768,256]{1,0:T(8,128)(2,1)S(1)} %get-tuple-element.36.tab_ref, f32[3,8,2048]{2,1,0:T(8,128)S(1)} %get-tuple-element.37.d_ref, f32[3,8,2048]{2,1,0:T(8,128)S(1)} %get-tuple-element.38.a_ref, ...), custom_call_target="tpu_custom_call" | custom-call | flops 4000000000 | bytes 10000000 | tf_op jit(solution)/shard_map/inner/pallas_call | solution.py:427
  39.9 0.0 collective-permute-done.2.refs_2_
  39.9 0.0 collective-permute-done.3.refs_3_
  40.0 0.0 collective-permute-done.4.refs_4_
  40.0 0.0 collective-permute-done.5.refs_5_
  40.0 0.0 collective-permute-done.7.refs_7_
  40.0 4.1 %tail.1 = (f32[1,2048]{1,0:T(1,128)}, f32[16,128]{1,0:T(8,128)}) custom-call(f32[216,128]{1,0:T(8,128)S(1)} %collective-permute-done.refs_0_, f32[216,128]{1,0:T(8,128)S(1)} %collective-permute-done.1.refs_1_, f32[216,128]{1,0:T(8,128)S(1)} %collective-permute-done.2.refs_2_, f32[216,128]{1,0:T(8,128)S(1)} %collective-permute-done.3.refs_3_, ...), custom_call_target="tpu_custom_call" | custom-call | tf_op jit(solution)/shard_map/tail/pallas_call | solution.py:439
Async XLA Ops:
  2.8 27.4 %collective-permute-start.6 = (f32[288,128]{1,0:T(8,128)S(1)}, f32[288,128]{1,0:T(8,128)S(1)}, u32[]{:S(2)}, u32[]{:S(2)}) collective-permute-start(f32[288,128]{1,0:T(8,128)S(1)} %get-tuple-element.35), channel_id=1, source_target_pairs={{0,8},{1,9},{2,10},{3,11},{4,12},{5,13},{6,14},{7,15},{8,0},{9,1},... | collective-permute-start | bytes 442376 | tf_op jit(solution)/shard_map/ppermute | solution.py:419
  10.6 14.4 %collective-permute-start = (f32[216,128]{1,0:T(8,128)S(1)}, f32[216,128]{1,0:T(8,128)S(1)}, u32[]{:S(2)}, u32[]{:S(2)}) collective-permute-start(f32[216,128]{1,0:T(8,128)S(1)} %get-tuple-element.29), channel_id=1, source_target_pairs={{0,2},{1,3},{2,4},{3,5},{4,6},{5,7},{6,8},{7,9},{8,10},{9,11},{10,... | collective-permute-start | bytes 331784 | tf_op jit(solution)/shard_map/ppermute | solution.py:423
  11.3 15.0 %collective-permute-start.1 = (f32[216,128]{1,0:T(8,128)S(1)}, f32[216,128]{1,0:T(8,128)S(1)}, u32[]{:S(2)}, u32[]{:S(2)}) collective-permute-start(f32[216,128]{1,0:T(8,128)S(1)} %get-tuple-element.30), channel_id=1, source_target_pairs={{0,4},{1,5},{2,6},{3,7},{4,8},{5,9},{6,10},{7,11},{8,12},{9,13},{1... | collective-permute-start | bytes 331784 | tf_op jit(solution)/shard_map/ppermute | solution.py:423
  12.5 27.4 %collective-permute-start.2 = (f32[216,128]{1,0:T(8,128)S(1)}, f32[216,128]{1,0:T(8,128)S(1)}, u32[]{:S(2)}, u32[]{:S(2)}) collective-permute-start(f32[216,128]{1,0:T(8,128)S(1)} %get-tuple-element.31), channel_id=1, source_target_pairs={{0,1},{1,2},{2,3},{3,4},{4,5},{5,6},{6,7},{7,8},{8,9},{9,10},{10,1... | collective-permute-start | bytes 331784 | tf_op jit(solution)/shard_map/ppermute | solution.py:423
  13.7 26.3 %collective-permute-start.3 = (f32[216,128]{1,0:T(8,128)S(1)}, f32[216,128]{1,0:T(8,128)S(1)}, u32[]{:S(2)}, u32[]{:S(2)}) collective-permute-start(f32[216,128]{1,0:T(8,128)S(1)} %get-tuple-element.32), channel_id=1, source_target_pairs={{0,255},{1,0},{2,1},{3,2},{4,3},{5,4},{6,5},{7,6},{8,7},{9,8},{10,... | collective-permute-start | bytes 331784 | tf_op jit(solution)/shard_map/ppermute | solution.py:423
  25.0 15.0 %collective-permute-start.4 = (f32[216,128]{1,0:T(8,128)S(1)}, f32[216,128]{1,0:T(8,128)S(1)}, u32[]{:S(2)}, u32[]{:S(2)}) collective-permute-start(f32[216,128]{1,0:T(8,128)S(1)} %get-tuple-element.33), channel_id=1, source_target_pairs={{0,252},{1,253},{2,254},{3,255},{4,0},{5,1},{6,2},{7,3},{8,4},{9,5... | collective-permute-start | bytes 331784 | tf_op jit(solution)/shard_map/ppermute | solution.py:423
  26.4 13.6 %collective-permute-start.5 = (f32[216,128]{1,0:T(8,128)S(1)}, f32[216,128]{1,0:T(8,128)S(1)}, u32[]{:S(2)}, u32[]{:S(2)}) collective-permute-start(f32[216,128]{1,0:T(8,128)S(1)} %get-tuple-element.34), channel_id=1, source_target_pairs={{0,254},{1,255},{2,0},{3,1},{4,2},{5,3},{6,4},{7,5},{8,6},{9,7},{1... | collective-permute-start | bytes 331784 | tf_op jit(solution)/shard_map/ppermute | solution.py:423
  30.2 9.8 %collective-permute-start.7 = (f32[288,128]{1,0:T(8,128)S(1)}, f32[288,128]{1,0:T(8,128)S(1)}, u32[]{:S(2)}, u32[]{:S(2)}) collective-permute-start(f32[288,128]{1,0:T(8,128)S(1)} %collective-permute-done.6.refs_6_), channel_id=1, source_target_pairs={{0,16},{1,17},{2,18},{3,19},{4,20},{5,21},{6,22},{7,23},{8,248},{9... | collective-permute-start | bytes 442376 | tf_op jit(solution)/shard_map/ppermute | solution.py:424

commit v3 on v2

--- a/solution.py
+++ b/solution.py
@@ -234,17 +234,22 @@
 FAR_ROWS = FAR_FACES + 144
 
 
-def inner_kernel(
-    tab_ref, d_ref, a_ref, p_ref, q_ref, k_ref, y_ref, s_ref, en_ref, if_ref, gy_ref, gp_ref, fo_ref, ao_ref, f_s, a_s, t_s
-):
-    nodes = node_tables(d_ref, a_ref)
+AHEAD = 4
+WIDTH = FACE_BLOCK * LANES
+
+
+def steps_ahead():
+    return jnp.where((lax.axis_index("dom") & 8) == 0, AHEAD, 0)
+
+
+def early_steps(first, last, total, tab_ref, p_ref, q_ref, k_ref, en_ref, if_ref, f_s, a_s, t_s):
     cells = cell_tables(p_ref, q_ref)
     perm = [k_ref[0:8, :], k_ref[8:16, :]]
-    width = FACE_BLOCK * LANES
-    t_s[:, :width] = jnp.zeros((2, width), jnp.float32)
+    before = pl.multiple_of(jnp.maximum(first - 1, 0) * WIDTH, WIDTH)
+    t_s[:, pl.ds(before, WIDTH)] = jnp.zeros((2, WIDTH), jnp.float32)
 
     def add(step, total):
-        cols = pl.ds(pl.multiple_of(step * width, width), width)
+        cols = pl.ds(pl.multiple_of(step * WIDTH, WIDTH), WIDTH)
         for side in range(2):
             total = total + scatter(if_ref[side : side + 1, cols], t_s[side : side + 1, cols])
         return total
@@ -255,7 +260,7 @@
         elem = en_ref[:, cols]
         own_corners(tab_ref, None, elem, ((0, 1), (2, 3), (4, 5), (6, 7)), (), f_s, a_s, cols)
         for face in range(FACE_BLOCK):
-            offset = pl.multiple_of(step * width + face * LANES, LANES)
+            offset = pl.multiple_of(step * WIDTH + face * LANES, LANES)
             ends = []
             for side in range(2):
                 lo, hi = split_index(if_ref[side : side + 1, pl.ds(offset, LANES)])
@@ -265,9 +270,29 @@
             t_s[1:2, pl.ds(offset, LANES)] = term_b
         return total
 
-    steps = FI // width
-    total = lax.fori_loop(0, steps, block, jnp.zeros((16, LANES), jnp.float32))
-    gp_ref[...] = add(steps - 1, total)
+    return add(last - 1, lax.fori_loop(first, last, block, total))
+
+
+def ahead_kernel(tab_ref, p_ref, q_ref, k_ref, y_ref, s_ref, en_ref, if_ref, gy_ref, gp_ref, f_s, a_s, t_s):
+    zero = jnp.zeros((OWN_CHUNKS, LANES), jnp.float32)
+    gp_ref[...] = zero
+    gy_ref[...] = jnp.zeros((1, AHEAD * LANES), jnp.float32)
+
+    @pl.when(steps_ahead() > 0)
+    def _():
+        gp_ref[...] = early_steps(0, AHEAD, zero, tab_ref, p_ref, q_ref, k_ref, en_ref, if_ref, f_s, a_s, t_s)
+        gy_ref[...] = -y_ref[:, : AHEAD * LANES] * strain_of(s_ref, f_s, a_s)
+
+
+def inner_kernel(
+    tab_ref, d_ref, a_ref, p_ref, q_ref, k_ref, y_ref, s_ref, en_ref, if_ref, gya_ref, gpa_ref,
+    gy_ref, gp_ref, fo_ref, ao_ref, f_s, a_s, t_s,
+):
+    nodes = node_tables(d_ref, a_ref)
+    first = steps_ahead()
+    gp_ref[...] = early_steps(
+        first, FI // WIDTH, gpa_ref[...], tab_ref, p_ref, q_ref, k_ref, en_ref, if_ref, f_s, a_s, t_s
+    )
 
     def late(step, _):
         start = pl.multiple_of(step * LANES, LANES)
@@ -280,6 +305,10 @@
 
     lax.fori_loop(0, EB // LANES, late, 0)
     gy_ref[...] = -y_ref[:, :OWN] * strain_of(s_ref, f_s, a_s)
+
+    @pl.when(first > 0)
+    def _():
+        gy_ref[:, : AHEAD * LANES] = gya_ref[...]
 
 
 def incoming(got, cells_ref, sc_ref, slots, i_s, t_s, start):
@@ -416,6 +445,19 @@
         stiffness,
     ) = packed[NEAR + 4 :]
     count = lax.axis_size("dom")
+    ahead_young, ahead_perm = pl.pallas_call(
+        ahead_kernel,
+        out_shape=[shape(1, AHEAD * LANES), shape(OWN_CHUNKS, LANES)],
+        scratch_shapes=[
+            pltpu.VMEM((192, AHEAD * LANES), jnp.float32),
+            pltpu.VMEM((192, AHEAD * LANES), jnp.float32),
+            pltpu.VMEM((2, AHEAD * WIDTH), jnp.float32),
+        ],
+        compiler_params=VMEM,
+        name="ahead",
+    )(table, pressure, adjoint_pressure, perm, young, stiffness, elem_nodes, inner_faces)
+    blocks = lax.optimization_barrier((*packed[: NEAR + 1], ahead_young, ahead_perm))
+    packed, (ahead_young, ahead_perm) = blocks[: NEAR + 1], blocks[NEAR + 1 :]
     swapped = lax.ppermute(packed[0], "dom", [(source, source ^ 8) for source in range(count)])
     near = []
     for number, j in enumerate(ORDER):
@@ -435,7 +477,7 @@
         compiler_params=VMEM,
         cost_estimate=pl.CostEstimate(flops=4 * 10**9, bytes_accessed=10**7, transcendentals=0),
         name="inner",
-    )(table, forward, adjoint, pressure, adjoint_pressure, perm, young, stiffness, elem_nodes, inner_faces)
+    )(table, forward, adjoint, pressure, adjoint_pressure, perm, young, stiffness, elem_nodes, inner_faces, ahead_young, ahead_perm)
     grad_young, grad_perm = pl.pallas_call(
         tail_kernel,
         out_shape=[shape(1, EL), shape(OWN_CHUNKS, LANES)],

time: 44.2 us -> 43.9 us (level)
  starting transfers between devices: 15.1 us -> 12.4 us
  waiting for transfers between devices: 12.3 us -> 13.9 us
  Pallas kernels: 16 us -> 16.7 us
    pallas_call x0 -> x1, Pallas kernels: none -> 3.54 us  [on_device(): pl.pallas_call(ahead_kernel, out_shape=[shape(1, AHEAD * LANES), shape(OW...]
    ppermute x1, starting transfers between devices: 7.81 us -> 4.3 us  [on_device(): lax.ppermute(packed[0], 'dom', [(source, source ^ 8) for source in range(...]
    pallas_call x1, Pallas kernels: 9.78 us -> 6.92 us  [on_device(): pl.pallas_call(inner_kernel, out_shape=[shape(1, OWN), shape(OWN_CHUNKS,...]
    ppermute x6, waiting for transfers between devices: 12.3 us -> 13.3 us  [on_device(): near.append(lax.ppermute(packed[number + 1], 'dom', pairs))]
    ppermute x6, starting transfers between devices: 7.24 us -> 8.14 us  [on_device(): near.append(lax.ppermute(packed[number + 1], 'dom', pairs))]
    ppermute x1, waiting for transfers between devices: 0.01 us -> 0.65 us  [on_device(): lax.ppermute(swapped, 'dom', [(source, (source - 16 if source & 8 else so...]
  transfers between devices with their start and end apart: 8 -> 8, of which waited for: 2 -> 3; matrix products, arithmetic and copies ran while one was open for 0% -> 0% of each run, Pallas kernels for 22% -> 16%
where the time goes in v3:
time: 43.9 us; the launch traced here: 43.8 us
  Pallas kernels  16.7 us (38%)
  waiting for transfers between devices  13.9 us (32%)
  starting transfers between devices  12.4 us (28%)
  between operations  0.69 us (2%)
    ppermute x6, waiting for transfers between devices, on_device(): near.append(lax.ppermute(packed[number + 1], 'dom', pairs))  13.3 us
    ppermute x6, starting transfers between devices, on_device(): near.append(lax.ppermute(packed[number + 1], 'dom', pairs))  8.14 us
    pallas_call x1, Pallas kernels, on_device(): pl.pallas_call(inner_kernel, out_shape=[shape(1, OWN), shape(OWN_CHUNKS,...  6.92 us
    ppermute x1, starting transfers between devices, on_device(): lax.ppermute(packed[0], 'dom', [(source, source ^ 8) for source in range(...  4.3 us
    pallas_call x1, Pallas kernels, on_device(): pl.pallas_call(tail_kernel, out_shape=[shape(1, EL), shape(OWN_CHUNKS, LA...  4.09 us
    pallas_call x1, Pallas kernels, on_device(): pl.pallas_call(ahead_kernel, out_shape=[shape(1, AHEAD * LANES), shape(OW...  3.54 us
    pallas_call x1, Pallas kernels, on_device(): pl.pallas_call(pack_kernel, out_shape=[shape(FAR_ROWS, LANES)] + [shape(R...  2.16 us
  transfers between devices with their start and end apart: 8, of which 3 were waited for; matrix products, arithmetic and copies ran while one was open for 0% of the time, Pallas kernels for 16%

profile of v3, /device:TPU:1, one launch (start us, length us, event | category | flops | bytes accessed | tf_op | source)
XLA Modules:
  0.0 43.8 jit_solution(14757543022006879270)
XLA Ops:
  0.6 2.2 %pack.1 = (f32[288,128]{1,0:T(8,128)S(1)}, f32[216,128]{1,0:T(8,128)S(1)}, f32[216,128]{1,0:T(8,128)S(1)}, f32[216,128]{1,0:T(8,128)S(1)}, f32[216,128]{1,0:T(8,...) custom-call(f32[8,2048]{1,0:T(8,128)} %refs_0_.1, ...), custom_call_target="tpu_custom_call" | custom-call | tf_op jit(solution)/shard_map/pack/pallas_call | solution.py:417
  2.8 3.5 %ahead.1 = (f32[1,512]{1,0:T(1,128)S(1)}, f32[16,128]{1,0:T(8,128)S(1)}) custom-call(bf16[768,256]{1,0:T(8,128)(2,1)S(1)} %get-tuple-element.47.tab_ref, f32[8,2048]{1,0:T(8,128)S(1)} %get-tuple-element.48.p_ref, f32[8,2048]{1,0:T(8,128)S(1)} %get-tuple-element.49.q_ref, f32[16,128]{1,0:T(8,128)S(1)} %get-tuple-element.50.k_ref, ...), custom_call_target="tpu_custom_call" | custom-call | tf_op jit(solution)/shard_map/ahead/pallas_call | solution.py:448
  6.3 4.3 %collective-permute-start.6 = (f32[288,128]{1,0:T(8,128)S(1)}, f32[288,128]{1,0:T(8,128)S(1)}, u32[]{:S(2)}, u32[]{:S(2)}) collective-permute-start(f32[288,128]{1,0:T(8,128)S(1)} %get-tuple-element.63), channel_id=1, source_target_pairs={{0,8},{1,9},{2,10},{3,11},{4,12},{5,13},{6,14},{7,15},{8,0},{9,1},... | collective-permute-start | bytes 442376 | tf_op jit(solution)/shard_map/ppermute | solution.py:461
  10.6 0.7 %collective-permute-start = (f32[216,128]{1,0:T(8,128)S(1)}, f32[216,128]{1,0:T(8,128)S(1)}, u32[]{:S(2)}, u32[]{:S(2)}) collective-permute-start(f32[216,128]{1,0:T(8,128)S(1)} %get-tuple-element.57), channel_id=1, source_target_pairs={{0,2},{1,3},{2,4},{3,5},{4,6},{5,7},{6,8},{7,9},{8,10},{9,11},{10,... | collective-permute-start | bytes 331784 | tf_op jit(solution)/shard_map/ppermute | solution.py:465
  11.4 1.2 %collective-permute-start.1 = (f32[216,128]{1,0:T(8,128)S(1)}, f32[216,128]{1,0:T(8,128)S(1)}, u32[]{:S(2)}, u32[]{:S(2)}) collective-permute-start(f32[216,128]{1,0:T(8,128)S(1)} %get-tuple-element.58), channel_id=1, source_target_pairs={{0,4},{1,5},{2,6},{3,7},{4,8},{5,9},{6,10},{7,11},{8,12},{9,13},{1... | collective-permute-start | bytes 331784 | tf_op jit(solution)/shard_map/ppermute | solution.py:465
  12.6 3.7 %collective-permute-start.2 = (f32[216,128]{1,0:T(8,128)S(1)}, f32[216,128]{1,0:T(8,128)S(1)}, u32[]{:S(2)}, u32[]{:S(2)}) collective-permute-start(f32[216,128]{1,0:T(8,128)S(1)} %get-tuple-element.59), channel_id=1, source_target_pairs={{0,1},{1,2},{2,3},{3,4},{4,5},{5,6},{6,7},{7,8},{8,9},{9,10},{10,1... | collective-permute-start | bytes 331784 | tf_op jit(solution)/shard_map/ppermute | solution.py:465
  16.3 0.0 collective-permute-start.3
  16.3 10.8 %collective-permute-done.refs_0_ = f32[216,128]{1,0:T(8,128)S(1)} collective-permute-done((f32[216,128]{1,0:T(8,128)S(1)}, f32[216,128]{1,0:T(8,128)S(1)}, u32[]{:S(2)}, u32[]{:S(2)}) %collective-permute-start) | collective-permute-done | bytes 110624 | tf_op jit(solution)/shard_map/ppermute | solution.py:465
  27.1 1.0 %collective-permute-start.4 = (f32[216,128]{1,0:T(8,128)S(1)}, f32[216,128]{1,0:T(8,128)S(1)}, u32[]{:S(2)}, u32[]{:S(2)}) collective-permute-start(f32[216,128]{1,0:T(8,128)S(1)} %get-tuple-element.61), channel_id=1, source_target_pairs={{0,252},{1,253},{2,254},{3,255},{4,0},{5,1},{6,2},{7,3},{8,4},{9,5... | collective-permute-start | bytes 331784 | tf_op jit(solution)/shard_map/ppermute | solution.py:465
  28.1 2.5 %collective-permute-done.1.refs_1_ = f32[216,128]{1,0:T(8,128)S(1)} collective-permute-done((f32[216,128]{1,0:T(8,128)S(1)}, f32[216,128]{1,0:T(8,128)S(1)}, u32[]{:S(2)}, u32[]{:S(2)}) %collective-permute-start.1) | collective-permute-done | bytes 110624 | tf_op jit(solution)/shard_map/ppermute | solution.py:465
  30.6 1.5 %collective-permute-start.5 = (f32[216,128]{1,0:T(8,128)S(1)}, f32[216,128]{1,0:T(8,128)S(1)}, u32[]{:S(2)}, u32[]{:S(2)}) collective-permute-start(f32[216,128]{1,0:T(8,128)S(1)} %get-tuple-element.62), channel_id=1, source_target_pairs={{0,254},{1,255},{2,0},{3,1},{4,2},{5,3},{6,4},{7,5},{8,6},{9,7},{1... | collective-permute-start | bytes 331784 | tf_op jit(solution)/shard_map/ppermute | solution.py:465
  32.0 0.0 collective-permute-done.6.refs_6_
  32.0 0.0 collective-permute-start.7
  32.0 6.9 %inner.1 = (f32[1,1536]{1,0:T(1,128)S(1)}, f32[16,128]{1,0:T(8,128)S(1)}, f32[192,512]{1,0:T(8,128)S(1)}, f32[192,512]{1,0:T(8,128)S(1)}) custom-call(bf16[768,256]{1,0:T(8,128)(2,1)S(1)} %get-tuple-element.47.tab_ref, f32[3,8,2048]{2,1,0:T(8,128)S(1)} %get-tuple-element.64.d_ref, f32[3,8,2048]{2,1,0:T(8,128)S(1)} %get-tuple-element.65.a_ref, ...), custom_call_target="tpu_custom_call" | custom-call | flops 4000000000 | bytes 10000000 | tf_op jit(solution)/shard_map/inner/pallas_call | solution.py:469
  39.0 0.0 collective-permute-done.2.refs_2_
  39.0 0.0 collective-permute-done.3.refs_3_
  39.0 0.0 collective-permute-done.4.refs_4_
  39.0 0.0 collective-permute-done.5.refs_5_
  39.0 0.6 %collective-permute-done.7.refs_7_ = f32[288,128]{1,0:T(8,128)S(1)} collective-permute-done((f32[288,128]{1,0:T(8,128)S(1)}, f32[288,128]{1,0:T(8,128)S(1)}, u32[]{:S(2)}, u32[]{:S(2)}) %collective-permute-start.7) | collective-permute-done | bytes 147488 | tf_op jit(solution)/shard_map/ppermute | solution.py:466
  39.7 4.1 %tail.1 = (f32[1,2048]{1,0:T(1,128)}, f32[16,128]{1,0:T(8,128)}) custom-call(f32[216,128]{1,0:T(8,128)S(1)} %collective-permute-done.refs_0_, f32[216,128]{1,0:T(8,128)S(1)} %collective-permute-done.1.refs_1_, f32[216,128]{1,0:T(8,128)S(1)} %collective-permute-done.2.refs_2_, f32[216,128]{1,0:T(8,128)S(1)} %collective-permute-done.3.refs_3_, ...), custom_call_target="tpu_custom_call" | custom-call | tf_op jit(solution)/shard_map/tail/pallas_call | solution.py:481
Async XLA Ops:
  6.3 25.7 %collective-permute-start.6 = (f32[288,128]{1,0:T(8,128)S(1)}, f32[288,128]{1,0:T(8,128)S(1)}, u32[]{:S(2)}, u32[]{:S(2)}) collective-permute-start(f32[288,128]{1,0:T(8,128)S(1)} %get-tuple-element.63), channel_id=1, source_target_pairs={{0,8},{1,9},{2,10},{3,11},{4,12},{5,13},{6,14},{7,15},{8,0},{9,1},... | collective-permute-start | bytes 442376 | tf_op jit(solution)/shard_map/ppermute | solution.py:461
  10.6 16.5 %collective-permute-start = (f32[216,128]{1,0:T(8,128)S(1)}, f32[216,128]{1,0:T(8,128)S(1)}, u32[]{:S(2)}, u32[]{:S(2)}) collective-permute-start(f32[216,128]{1,0:T(8,128)S(1)} %get-tuple-element.57), channel_id=1, source_target_pairs={{0,2},{1,3},{2,4},{3,5},{4,6},{5,7},{6,8},{7,9},{8,10},{9,11},{10,... | collective-permute-start | bytes 331784 | tf_op jit(solution)/shard_map/ppermute | solution.py:465
  11.4 19.2 %collective-permute-start.1 = (f32[216,128]{1,0:T(8,128)S(1)}, f32[216,128]{1,0:T(8,128)S(1)}, u32[]{:S(2)}, u32[]{:S(2)}) collective-permute-start(f32[216,128]{1,0:T(8,128)S(1)} %get-tuple-element.58), channel_id=1, source_target_pairs={{0,4},{1,5},{2,6},{3,7},{4,8},{5,9},{6,10},{7,11},{8,12},{9,13},{1... | collective-permute-start | bytes 331784 | tf_op jit(solution)/shard_map/ppermute | solution.py:465
  12.6 26.4 %collective-permute-start.2 = (f32[216,128]{1,0:T(8,128)S(1)}, f32[216,128]{1,0:T(8,128)S(1)}, u32[]{:S(2)}, u32[]{:S(2)}) collective-permute-start(f32[216,128]{1,0:T(8,128)S(1)} %get-tuple-element.59), channel_id=1, source_target_pairs={{0,1},{1,2},{2,3},{3,4},{4,5},{5,6},{6,7},{7,8},{8,9},{9,10},{10,1... | collective-permute-start | bytes 331784 | tf_op jit(solution)/shard_map/ppermute | solution.py:465
  16.3 22.7 %collective-permute-start.3 = (f32[216,128]{1,0:T(8,128)S(1)}, f32[216,128]{1,0:T(8,128)S(1)}, u32[]{:S(2)}, u32[]{:S(2)}) collective-permute-start(f32[216,128]{1,0:T(8,128)S(1)} %get-tuple-element.60), channel_id=1, source_target_pairs={{0,255},{1,0},{2,1},{3,2},{4,3},{5,4},{6,5},{7,6},{8,7},{9,8},{10,... | collective-permute-start | bytes 331784 | tf_op jit(solution)/shard_map/ppermute | solution.py:465
  27.1 11.9 %collective-permute-start.4 = (f32[216,128]{1,0:T(8,128)S(1)}, f32[216,128]{1,0:T(8,128)S(1)}, u32[]{:S(2)}, u32[]{:S(2)}) collective-permute-start(f32[216,128]{1,0:T(8,128)S(1)} %get-tuple-element.61), channel_id=1, source_target_pairs={{0,252},{1,253},{2,254},{3,255},{4,0},{5,1},{6,2},{7,3},{8,4},{9,5... | collective-permute-start | bytes 331784 | tf_op jit(solution)/shard_map/ppermute | solution.py:465
  30.6 8.4 %collective-permute-start.5 = (f32[216,128]{1,0:T(8,128)S(1)}, f32[216,128]{1,0:T(8,128)S(1)}, u32[]{:S(2)}, u32[]{:S(2)}) collective-permute-start(f32[216,128]{1,0:T(8,128)S(1)} %get-tuple-element.62), channel_id=1, source_target_pairs={{0,254},{1,255},{2,0},{3,1},{4,2},{5,3},{6,4},{7,5},{8,6},{9,7},{1... | collective-permute-start | bytes 331784 | tf_op jit(solution)/shard_map/ppermute | solution.py:465
  32.0 7.6 %collective-permute-start.7 = (f32[288,128]{1,0:T(8,128)S(1)}, f32[288,128]{1,0:T(8,128)S(1)}, u32[]{:S(2)}, u32[]{:S(2)}) collective-permute-start(f32[288,128]{1,0:T(8,128)S(1)} %collective-permute-done.6.refs_6_), channel_id=1, source_target_pairs={{0,16},{1,17},{2,18},{3,19},{4,20},{5,21},{6,22},{7,23},{8,248},{9... | collective-permute-start | bytes 442376 | tf_op jit(solution)/shard_map/ppermute | solution.py:466
